TPU v7x, 32 devices: a whole 2x2x4 slice. The times are simulated.
32 devices in a mesh: shot: 4 (over y, core), tile: 8 (over z, x).
Axes of the slice: x: 2, y: 2, z: 4, core: 2. Of those that a mesh axis runs over, the one named last changes fastest.
Arguments:
- source: bfloat16 [64, 1, 32, 32, 128], P(('shot', 'tile')), may hold values from -6 to 6
- receiver: bfloat16 [64, 1, 32, 32, 128], P(('shot', 'tile')), may hold values from -6 to 6
- corners: int32 [64, 2], P(('shot', 'tile')), may hold values from 0 to 224, as said below
Outputs:
- filtered: float32 [32, 256, 256], P('tile', 'shot')
Inputs may be any that keep to these rules, and one draw needn't show every extreme that they name: corners[s, 0] is at most 224 and corners[s, 1] at most 128, so every box lies inside the image.
All inputs are finite; a program needn't handle non-finite values.
Results may differ from a plain program's by a relative error of at most 0.0003.
Values may be sent and summed in bfloat16 or wider, within the bound.
No kernel may reach another device: no remote copies, remote signals or barrier semaphores. Data moves between devices by JAX's collectives and lax.ppermute only.
A program may use at most 64 MiB of HBM per device.

v0:
```python
import jax
import jax.numpy as jnp
from jax import lax
from jax.sharding import PartitionSpec as P

X = 256
Y = 256


damping = 1.0


def with_halo(cells, sides, width):
    for axis, dim in sides:
        count = lax.axis_size(axis)
        ends = count - 1
        head = lax.slice_in_dim(cells, 0, width, axis=dim)
        tail = lax.slice_in_dim(cells, cells.shape[dim] - width, cells.shape[dim], axis=dim)
        cells = jnp.concatenate(
            [
                lax.ppermute(tail, axis, [(i, (i + 1) % count) for i in range(ends)]),
                cells,
                lax.ppermute(head, axis, [((i + 1) % count, i) for i in range(ends)]),
            ],
            axis=dim,
        )
    return cells


def laplace(padded):
    center = padded[1:-1, 1:-1, 1:-1]
    beside = padded[2:, 1:-1, 1:-1] + padded[:-2, 1:-1, 1:-1]
    beside = beside + padded[1:-1, 2:, 1:-1] + padded[1:-1, :-2, 1:-1]
    beside = beside + padded[1:-1, 1:-1, 2:] + padded[1:-1, 1:-1, :-2]
    return beside - 6.0 * center


def correlate(wave_bf, back_bf, time_axis):
    wave = wave_bf.astype(jnp.float32)
    back = back_bf.astype(jnp.float32)
    return jnp.stack((jnp.sum(wave * back, axis=time_axis), jnp.sum(wave * wave, axis=time_axis)))


def per_device(source, receiver, corners):
    tile_count = lax.axis_size("tile")
    slab_depth = source.shape[2] // tile_count
    box_rows = source.shape[3]
    box_cols = source.shape[4]
    got_wave, got_back = (
        lax.all_to_all(source, "tile", split_axis=2, concat_axis=0, tiled=True),
        lax.all_to_all(receiver, "tile", split_axis=2, concat_axis=0, tiled=True),
    )
    stacked = correlate(got_wave, got_back, 1)
    corner_all = lax.all_gather(corners, "tile", axis=0, tiled=True)
    col_index = jnp.arange(Y, dtype=jnp.int32)
    box_col = jnp.arange(box_cols, dtype=jnp.int32)
    col_table = (
        col_index[None, None, :] == corner_all[:, 1][:, None, None] + box_col[None, :, None]
    ).astype(jnp.float32)
    placed = jnp.einsum("qkzab,kby->qzkay", stacked, col_table, precision=lax.Precision.HIGHEST)
    shots_in = corner_all.shape[0]
    placed = placed.reshape(2, slab_depth, shots_in * box_rows, Y)
    row_target = (
        corner_all[:, 0][:, None] + jnp.arange(box_rows, dtype=jnp.int32)[None, :]
    ).reshape(-1)
    row_index = jnp.arange(X, dtype=jnp.int32)
    row_table = (row_target[:, None] == row_index[None, :]).astype(jnp.float32)
    sums = jnp.einsum("rx,qzry->qzxy", row_table, placed, precision=lax.Precision.HIGHEST)
    image_part = sums[0]
    light_part = sums[1]
    image_sum, light_sum = (
        lax.psum_scatter(image_part, "shot", scatter_dimension=1, tiled=True),
        lax.psum_scatter(light_part, "shot", scatter_dimension=1, tiled=True),
    )
    normal = image_sum / (damping + light_sum)
    padded = with_halo(normal, (("shot", 1), ("tile", 0)), 1)
    padded = jnp.pad(padded, ((0, 0), (0, 0), (1, 1)))
    return laplace(padded)


def solution(mesh):
    return jax.shard_map(
        per_device,
        mesh=mesh,
        in_specs=(
            P(("shot", "tile"), None, None, None, None),
            P(("shot", "tile"), None, None, None, None),
            P(("shot", "tile"), None),
        ),
        out_specs=P("tile", "shot", None),
        check_vma=False,
    )
```

profile of v0, /device:TPU:3, one launch (start us, length us, event | category | flops | bytes accessed | tf_op | source)
XLA Modules:
  0.0 143.1 jit_solution(10602599561009317554)
XLA Ops:
  6.5 2.0 %copy.15 = bf16[2,1,32,32,128]{4,3,1,0,2:T(8,128)(2,1)} copy(bf16[2,1,32,32,128]{4,3,2,1,0:T(8,128)(2,1)} %param.3) | data formatting | bytes 1048576 | tf_op args[0]
  8.5 5.8 %all-to-all-start = ((bf16[2,1,32,32,128]{4,3,1,0,2:T(8,128)(2,1)}), bf16[2,1,32,32,128]{4,3,1,0,2:T(8,128)(2,1)S(1)}, u32[]{:S(2)}, u32[]{:S(2)}) async-start(bf16[2,1,32,32,128]{4,3,1,0,2:T(8,128)(2,1)} %copy.15), calls=%async_computation | async-start | bytes 1048576 | tf_op jit(solution)/shard_map/all_to_all | solution.py:50
  14.3 0.9 copy.16
  15.2 12.9 %all-to-all-done = bf16[2,1,32,32,128]{4,3,1,0,2:T(8,128)(2,1)S(1)} async-done(((bf16[2,1,32,32,128]{4,3,1,0,2:T(8,128)(2,1)}), bf16[2,1,32,32,128]{4,3,1,0,2:T(8,128)(2,1)S(1)}, u32[]{:S(2)}, u32[]{:S(2)}) %all-to-all-start) | async-done | bytes 524320 | tf_op jit(solution)/shard_map/all_to_all | solution.py:50
  28.1 4.5 %all-to-all-start.1 = ((bf16[2,1,32,32,128]{4,3,1,0,2:T(8,128)(2,1)}), bf16[2,1,32,32,128]{4,3,1,0,2:T(8,128)(2,1)S(1)}, u32[]{:S(2)}, u32[]{:S(2)}) async-start(bf16[2,1,32,32,128]{4,3,1,0,2:T(8,128)(2,1)} %copy.16), calls=%async_computation.1 | async-start | bytes 1048576 | tf_op jit(solution)/shard_map/all_to_all | solution.py:51
  32.6 19.9 %all-gather = s32[8,2,2]{2,1,0:T(2,128)S(1)} all-gather(s32[1,2,2]{2,1,0:T(2,128)S(1)} %bitcast.41), channel_id=1, replica_groups=mesh['shot'=4,'tile'=8] {'tile'}, dimensions={0}, use_global_device_ids=true | all-gather | bytes 144 | tf_op jit(solution)/shard_map/all_gather | solution.py:54
  52.5 0.1 fusion.17
  52.6 0.1 copy.29
  52.7 0.1 copy.28
  52.7 0.1 iota_add_fusion
  52.8 0.1 add.74
  52.9 0.1 iota_add_fusion.1
  53.0 0.3 convert_multiply_fusion.1
  53.4 2.3 %convolution_bitcast_fusion = f32[2,4,16,32,256]{4,3,1,0,2:T(8,128)S(1)} fusion(f32[1,16,4,32,128]{4,3,2,0,1:T(8,128)S(1)} %bitcast.37, f32[1,16,4,32,128]{4,3,2,0,1:T(8,128)S(1)} %bitcast.36, s32[16,128]{1,0:T(8,128)S(1)} %iota_add_fusion.1), kind=kOutput, calls=%fused_computation | convolution fusion | flops 1611661312 | bytes 6299648 | tf_op jit(solution)/shard_map/qkzab,kby->qzkay/dot_general | solution.py:60
  55.7 0.6 copy.19
  56.3 3.6 %convolution_bitcast_fusion.1 = f32[2,4,256,256]{2,3,1,0:T(8,128)S(1)} fusion(f32[2,4,512,256]{3,2,1,0:T(8,128)S(1)} %bitcast.33, s32[512]{0:T(512)S(1)} %add.74), kind=kOutput, calls=%fused_computation.6 | convolution fusion | flops 3221356544 | bytes 6293504 | tf_op jit(solution)/shard_map/rx,qzry->qzxy/dot_general | solution.py:68
  60.0 0.2 slice_bitcast_fusion.1
  60.2 1.3 copy.21
  61.5 1.3 copy.22
  62.9 0.6 dynamic-slice
  64.1 51.9 %all-reduce.6.cloned.1.call-done = (f32[4,256,256]{2,0,1:T(4,128)}, f32[4,256,256]{2,0,1:T(4,128)}) async-done(((f32[4,256,256]{2,0,1:T(4,128)}, f32[4,256,256]{2,0,1:T(4,128)}), (f32[4,256,256]{2,0,1:T(4,128)}, f32[4,256,256]{2,0,1:T(4,128)})) %all-reduce.6.cloned.1.call-update) | async-done | bytes 2097168
  116.0 1.1 fusion.13
  117.1 3.1 %collective-permute-start = (f32[4,1,256]{2,0,1:T(4,128)S(1)}, f32[4,1,256]{2,0,1:T(4,128)S(1)}, u32[]{:S(2)}, u32[]{:S(2)}) collective-permute-start(f32[4,1,256]{2,0,1:T(4,128)S(1)} %get-tuple-element.13), channel_id=1, source_target_pairs={{0,8},{8,16},{16,24},{1,9},{9,17},{17,25},{2,10},{10,18},{18,26},{... | collective-permute-start | bytes 12296 | tf_op jit(solution)/shard_map/ppermute | solution.py:21
  120.2 1.9 %collective-permute-start.1 = (f32[4,1,256]{2,0,1:T(4,128)S(1)}, f32[4,1,256]{2,0,1:T(4,128)S(1)}, u32[]{:S(2)}, u32[]{:S(2)}) collective-permute-start(f32[4,1,256]{2,0,1:T(4,128)S(1)} %get-tuple-element.14), channel_id=1, source_target_pairs={{8,0},{16,8},{24,16},{9,1},{17,9},{25,17},{10,2},{18,10},{26,18},{... | collective-permute-start | bytes 12296 | tf_op jit(solution)/shard_map/ppermute | solution.py:23
  122.1 3.0 %collective-permute-done.1 = f32[4,1,256]{2,0,1:T(4,128)S(1)} collective-permute-done((f32[4,1,256]{2,0,1:T(4,128)S(1)}, f32[4,1,256]{2,0,1:T(4,128)S(1)}, u32[]{:S(2)}, u32[]{:S(2)}) %collective-permute-start.1) | collective-permute-done | bytes 4128 | tf_op jit(solution)/shard_map/ppermute | solution.py:23
  125.1 0.1 pad_maximum_fusion.8
  125.2 3.1 %collective-permute-start.3 = (f32[1,66,256]{2,0,1:T(1,128)S(1)}, f32[1,66,256]{2,0,1:T(1,128)S(1)}, u32[]{:S(2)}, u32[]{:S(2)}) collective-permute-start(f32[1,66,256]{2,0,1:T(1,128)S(1)} %get-tuple-element.11), channel_id=1, source_target_pairs={{0,1},{1,2},{2,3},{3,4},{4,5},{5,6},{6,7},{8,9},{9,10},{10,11},{11... | collective-permute-start | bytes 202760 | tf_op jit(solution)/shard_map/ppermute | solution.py:21
  128.3 2.2 %collective-permute-start.2 = (f32[1,66,256]{2,0,1:T(1,128)S(1)}, f32[1,66,256]{2,0,1:T(1,128)S(1)}, u32[]{:S(2)}, u32[]{:S(2)}) collective-permute-start(f32[1,66,256]{2,0,1:T(1,128)S(1)} %get-tuple-element.12), channel_id=1, source_target_pairs={{1,0},{2,1},{3,2},{4,3},{5,4},{6,5},{7,6},{9,8},{10,9},{11,10},{12... | collective-permute-start | bytes 202760 | tf_op jit(solution)/shard_map/ppermute | solution.py:23
  130.5 3.7 %collective-permute-done.2 = f32[1,66,256]{2,0,1:T(1,128)S(1)} collective-permute-done((f32[1,66,256]{2,0,1:T(1,128)S(1)}, f32[1,66,256]{2,0,1:T(1,128)S(1)}, u32[]{:S(2)}, u32[]{:S(2)}) %collective-permute-start.2) | collective-permute-done | bytes 67616 | tf_op jit(solution)/shard_map/ppermute | solution.py:23
  134.3 0.7 select_maximum_fusion
  135.0 0.5 fusion.9
  135.5 0.8 copy.23
  (14 shorter events, 0.2 us)
Async XLA Ops:
  6.5 7.8 %copy-start = (bf16[2,1,32,32,128]{4,3,2,1,0:T(8,128)(2,1)S(1)}, bf16[2,1,32,32,128]{4,3,2,1,0:T(8,128)(2,1)}, u32[]{:S(2)}) copy-start(bf16[2,1,32,32,128]{4,3,2,1,0:T(8,128)(2,1)} %param.4) | copy-start | bytes 1572868
  6.5 26.1 %copy-start.1 = (s32[2,2]{1,0:T(2,128)S(1)}, s32[2,2]{1,0:T(2,128)}, u32[]{:S(2)}) copy-start(s32[2,2]{1,0:T(2,128)} %param.5) | copy-start | bytes 52
  8.5 19.5 %all-to-all-start = ((bf16[2,1,32,32,128]{4,3,1,0,2:T(8,128)(2,1)}), bf16[2,1,32,32,128]{4,3,1,0,2:T(8,128)(2,1)S(1)}, u32[]{:S(2)}, u32[]{:S(2)}) async-start(bf16[2,1,32,32,128]{4,3,1,0,2:T(8,128)(2,1)} %copy.15), calls=%async_computation | async-start | bytes 1048576 | tf_op jit(solution)/shard_map/all_to_all | solution.py:50
  28.1 24.9 %all-to-all-start.1 = ((bf16[2,1,32,32,128]{4,3,1,0,2:T(8,128)(2,1)}), bf16[2,1,32,32,128]{4,3,1,0,2:T(8,128)(2,1)S(1)}, u32[]{:S(2)}, u32[]{:S(2)}) async-start(bf16[2,1,32,32,128]{4,3,1,0,2:T(8,128)(2,1)} %copy.16), calls=%async_computation.1 | async-start | bytes 1048576 | tf_op jit(solution)/shard_map/all_to_all | solution.py:51
  32.6 83.4 %all-reduce.6.cloned.1.call-start = ((), (), s32[]{:S(2)}) async-start(), calls=%async_computation.2 | async-start | bytes 4194304
  61.5 1.3 copy-start.2
  117.1 5.0 %collective-permute-start = (f32[4,1,256]{2,0,1:T(4,128)S(1)}, f32[4,1,256]{2,0,1:T(4,128)S(1)}, u32[]{:S(2)}, u32[]{:S(2)}) collective-permute-start(f32[4,1,256]{2,0,1:T(4,128)S(1)} %get-tuple-element.13), channel_id=1, source_target_pairs={{0,8},{8,16},{16,24},{1,9},{9,17},{17,25},{2,10},{10,18},{18,26},{... | collective-permute-start | bytes 12296 | tf_op jit(solution)/shard_map/ppermute | solution.py:21
  120.2 4.9 %collective-permute-start.1 = (f32[4,1,256]{2,0,1:T(4,128)S(1)}, f32[4,1,256]{2,0,1:T(4,128)S(1)}, u32[]{:S(2)}, u32[]{:S(2)}) collective-permute-start(f32[4,1,256]{2,0,1:T(4,128)S(1)} %get-tuple-element.14), channel_id=1, source_target_pairs={{8,0},{16,8},{24,16},{9,1},{17,9},{25,17},{10,2},{18,10},{26,18},{... | collective-permute-start | bytes 12296 | tf_op jit(solution)/shard_map/ppermute | solution.py:23
  125.2 5.3 %collective-permute-start.3 = (f32[1,66,256]{2,0,1:T(1,128)S(1)}, f32[1,66,256]{2,0,1:T(1,128)S(1)}, u32[]{:S(2)}, u32[]{:S(2)}) collective-permute-start(f32[1,66,256]{2,0,1:T(1,128)S(1)} %get-tuple-element.11), channel_id=1, source_target_pairs={{0,1},{1,2},{2,3},{3,4},{4,5},{5,6},{6,7},{8,9},{9,10},{10,11},{11... | collective-permute-start | bytes 202760 | tf_op jit(solution)/shard_map/ppermute | solution.py:21
  128.3 5.9 %collective-permute-start.2 = (f32[1,66,256]{2,0,1:T(1,128)S(1)}, f32[1,66,256]{2,0,1:T(1,128)S(1)}, u32[]{:S(2)}, u32[]{:S(2)}) collective-permute-start(f32[1,66,256]{2,0,1:T(1,128)S(1)} %get-tuple-element.12), channel_id=1, source_target_pairs={{1,0},{2,1},{3,2},{4,3},{5,4},{6,5},{7,6},{9,8},{10,9},{11,10},{12... | collective-permute-start | bytes 202760 | tf_op jit(solution)/shard_map/ppermute | solution.py:23
Sparse Core Ops, SparseCore 0:
  63.0 52.9 all-reduce.5
where the time goes:
time: 143 us
  waiting for transfers between devices  71.5 us (50%)
  starting transfers between devices  20.6 us (14%)
  blocking collectives  19.9 us (14%)
  between operations  14.2 us (10%)
  local copies, waits for them, and re-layouts  8.1 us (6%)
  matrix products  5.91 us (4%)
  other arithmetic  2.88 us (2%)
    unnamed x2, waiting for transfers between devices  51.9 us
    all_gather x1, blocking collectives, per_device(): corner_all = lax.all_gather(corners, 'tile', axis=0, tiled=True)  19.9 us
    all_to_all x1, waiting for transfers between devices, per_device(): lax.all_to_all(source, 'tile', split_axis=2, concat_axis=0, tiled=True)  12.9 us
    ppermute x2, waiting for transfers between devices, with_halo(): lax.ppermute(head, axis, [((i + 1) % count, i) for i in range(ends)])  6.73 us
    ppermute x2, starting transfers between devices, with_halo(): lax.ppermute(tail, axis, [(i, (i + 1) % count) for i in range(ends)])  6.16 us
    all_to_all x1, starting transfers between devices, per_device(): lax.all_to_all(source, 'tile', split_axis=2, concat_axis=0, tiled=True)  5.78 us
    all_to_all x1, starting transfers between devices, per_device(): lax.all_to_all(receiver, 'tile', split_axis=2, concat_axis=0, tiled=True)  4.54 us
    ppermute x2, starting transfers between devices, with_halo(): lax.ppermute(head, axis, [((i + 1) % count, i) for i in range(ends)])  4.09 us
  transfers between devices with their start and end apart: 7, of which 4 were waited for; matrix products, arithmetic and copies ran while one was open for 1% of the time, Pallas kernels for 0%

commit v1 on v0

v1 whole, which is shorter than its diff:
```python
import functools

import jax
import jax.numpy as jnp
from jax import lax
from jax.experimental import pallas as pl
from jax.experimental.pallas import tpu as pltpu
from jax.sharding import Mesh, PartitionSpec as P

X = 256
Y = 256
LANES = 128
CORES = 2
EDGE = 8

damping = 1.0


def whole(count):
    return [pl.BlockSpec(memory_space=pltpu.VMEM)] * count


def place_kernel(dims, corner_ref, spot_ref, got_ref, *refs):
    shots, times, planes, rows, sides, half = dims
    outs, total = refs[:-1], refs[-1]
    senders = got_ref.shape[0]
    field = shots * times * planes * rows
    total[...] = jnp.zeros_like(total)
    lane = lax.broadcasted_iota(jnp.int32, (rows, LANES), 1)

    def one_sender(sender, carry):
        for shot in range(shots):
            row = corner_ref[sender, 2 * shot]
            col = corner_ref[sender, 2 * shot + 1]
            turn = lax.rem(col, LANES)
            first = lane >= col
            sums = []
            for plane in range(planes):
                image = light = None
                for time in range(times):
                    at = ((shot * times + time) * planes + plane) * rows
                    wave = got_ref[sender, at:at + rows, :].astype(jnp.float32)
                    back = got_ref[sender, field + at:field + at + rows, :].astype(jnp.float32)
                    image = wave * back if image is None else image + wave * back
                    light = wave * wave if light is None else light + wave * wave
                sums.append((0, plane, pltpu.roll(image, turn, 1)))
                sums.append((1, plane, pltpu.roll(light, turn, 1)))
            span = pl.ds(row, rows)
            fresh = []
            for kind, plane, value in sums:
                low = total[0, kind, plane, span, :]
                high = total[1, kind, plane, span, :]
                fresh.append((kind, plane, low + jnp.where(first, value, 0.0), high + jnp.where(first, 0.0, value)))
            for kind, plane, low, high in fresh:
                total[0, kind, plane, span, :] = low
                total[1, kind, plane, span, :] = high
        return carry

    lax.fori_loop(0, senders, one_sender, 0)
    side = spot_ref[0]
    slot = lax.broadcasted_iota(jnp.int32, (EDGE, LANES), 0)
    for step, out in enumerate(outs):
        target = lax.rem(side + step, sides)
        start = pl.multiple_of(target * half, half)
        before = pl.multiple_of(lax.max(start - EDGE, 0), EDGE)
        after = pl.multiple_of(lax.min(start + half, X - EDGE), EDGE)
        for kind in range(2):
            for plane in range(planes):
                for tile in range(Y // LANES):
                    lanes = slice(tile * LANES, (tile + 1) * LANES)
                    out[kind, plane, :half, lanes] = total[tile, kind, plane, pl.ds(start, half), :]
                    above = total[tile, kind, plane, pl.ds(before, EDGE), :]
                    below = total[tile, kind, plane, pl.ds(after, EDGE), :]
                    above = jnp.where(target > 0, above, 0.0)
                    below = jnp.where(target < sides - 1, below, 0.0)
                    pair = jnp.where(slot == EDGE - 1, above, jnp.where(slot == 0, below, 0.0))
                    out[kind, plane, half:, lanes] = pair


def normal_kernel(dims, spot_ref, *refs):
    planes, half, parts = dims
    ins, (keep, give, straight, across, whole_ref) = refs[:parts], refs[parts:]
    strip = half // CORES
    core = spot_ref[1]
    image = ins[0][0]
    light = ins[0][1]
    for part in ins[1:]:
        image = image + part[0]
        light = light + part[1]
    whole_ref[...] = image / (damping + light)
    slot = lax.broadcasted_iota(jnp.int32, (EDGE, Y), 0)
    edge_plane = core * (planes - 1)
    for out, lone, which in ((keep, straight, core), (give, across, 1 - core)):
        start = pl.multiple_of(which * strip, strip)
        before = pl.multiple_of(lax.max(start - EDGE, 0), EDGE)
        after = pl.multiple_of(lax.min(start + strip, half - EDGE), EDGE)
        for plane in range(planes):
            out[plane, :strip, :] = whole_ref[plane, pl.ds(start, strip), :]
            far = whole_ref[plane, half:, :]
            above = jnp.where(which > 0, whole_ref[plane, pl.ds(before, EDGE), :], far)
            below = jnp.where(which < CORES - 1, whole_ref[plane, pl.ds(after, EDGE), :], far)
            out[plane, strip:, :] = jnp.where(slot == EDGE - 1, above, jnp.where(slot == 0, below, 0.0))
        lone[...] = whole_ref[edge_plane, pl.ds(start, strip), :]


def laplace_kernel(dims, spot_ref, keep, got, straight, across, out):
    planes, strip = dims
    core = spot_ref[1]
    row = lax.broadcasted_iota(jnp.int32, (strip, Y), 0)
    col = lax.broadcasted_iota(jnp.int32, (strip, Y), 1)

    def lateral(cells):
        body = cells[:strip]
        above = jnp.where(row == 0, cells[strip + EDGE - 1:strip + EDGE], pltpu.roll(body, 1, 0))
        below = jnp.where(row == strip - 1, cells[strip:strip + 1], pltpu.roll(body, strip - 1, 0))
        left = jnp.where(col == 0, 0.0, pltpu.roll(body, 1, 1))
        right = jnp.where(col == Y - 1, 0.0, pltpu.roll(body, Y - 1, 1))
        return above + below + left + right - 6.0 * body

    upper_first = core == 0
    lower = jnp.where(upper_first, across[...], straight[...])
    upper = jnp.where(upper_first, straight[...], across[...])
    depth = planes * CORES
    base = core * planes
    other = (1 - core) * planes
    for ref, at in ((keep, base), (got, other)):
        for plane in range(planes):
            out[at + plane] = lateral(ref[plane])
    for ref, far, at in ((keep, got, base), (got, keep, other)):
        lowest = at == 0
        for plane in range(planes):
            if plane == 0:
                down = jnp.where(lowest, lower, far[planes - 1, :strip, :])
            else:
                down = ref[plane - 1, :strip, :]
            if plane == planes - 1:
                up = jnp.where(lowest, far[0, :strip, :], upper)
            else:
                up = ref[plane + 1, :strip, :]
            out[at + plane] = out[at + plane] + (down + up)


def per_device(source, receiver, corners):
    sides = lax.axis_size("side")
    tiles = lax.axis_size("tile")
    spread = tiles * CORES
    shots, times, depth, rows, cols = source.shape
    planes = depth // spread
    half = X // sides
    strip = half // CORES
    side = lax.axis_index("side")
    core = lax.axis_index("core")
    spot = jnp.stack([side, core]).astype(jnp.int32)

    fields = [
        field.reshape(shots, times, spread, planes, rows, cols).transpose(2, 0, 1, 3, 4, 5).reshape(spread, -1, cols)
        for field in (source, receiver)
    ]
    tag = jnp.pad(corners.astype(jnp.bfloat16).reshape(1, -1), ((0, 15), (0, cols - 2 * shots)))
    tag = jnp.broadcast_to(tag[None], (spread, 16, cols))
    packed = jnp.concatenate(fields + [tag], axis=1)
    got = lax.all_to_all(packed, ("tile", "core"), split_axis=0, concat_axis=0, tiled=True)
    corner_all = got[:, -16, : 2 * shots].astype(jnp.int32)

    smem = pl.BlockSpec(memory_space=pltpu.SMEM)
    part_shape = jax.ShapeDtypeStruct((2, planes, half + EDGE, Y), jnp.float32)
    parts = pl.pallas_call(
        functools.partial(place_kernel, (shots, times, planes, rows, sides, half)),
        out_shape=[part_shape] * sides,
        in_specs=[smem, smem] + whole(1),
        out_specs=whole(sides),
        scratch_shapes=[pltpu.VMEM((Y // LANES, 2, planes, X, LANES), jnp.float32)],
    )(corner_all, spot, got)
    parts = [parts[0]] + [
        lax.ppermute(parts[step], "side", [(i, (i + step) % sides) for i in range(sides)])
        for step in range(1, sides)
    ]

    strip_shape = jax.ShapeDtypeStruct((planes, strip + EDGE, Y), jnp.float32)
    plane_shape = jax.ShapeDtypeStruct((strip, Y), jnp.float32)
    keep, give, straight, across = pl.pallas_call(
        functools.partial(normal_kernel, (planes, half, sides)),
        out_shape=[strip_shape, strip_shape, plane_shape, plane_shape],
        in_specs=[smem] + whole(sides),
        out_specs=whole(4),
        scratch_shapes=[pltpu.VMEM((planes, half + EDGE, Y), jnp.float32)],
    )(spot, *parts)
    at = lambda c, t: c * tiles + t
    swap = [(at(c, t), at(1 - c, t)) for c in range(CORES) for t in range(tiles)]
    along = [(at(0, t), at(0, t - 1)) for t in range(1, tiles)]
    along += [(at(1, t), at(1, t + 1)) for t in range(tiles - 1)]
    cross = [(at(0, t), at(1, t - 1)) for t in range(1, tiles)]
    cross += [(at(1, t), at(0, t + 1)) for t in range(tiles - 1)]
    names = ("core", "tile")
    straight = lax.ppermute(straight, names, along)
    across = lax.ppermute(across, names, cross)
    got_strip = lax.ppermute(give, names, swap)
    return pl.pallas_call(
        functools.partial(laplace_kernel, (planes, strip)),
        out_shape=jax.ShapeDtypeStruct((planes * CORES, strip, Y), jnp.float32),
        in_specs=[smem] + whole(4),
        out_specs=pl.BlockSpec(memory_space=pltpu.VMEM),
    )(spot, keep, got_strip, straight, across)


def solution(mesh):
    shot_count, tile_count = mesh.devices.shape
    fine = Mesh(mesh.devices.reshape(shot_count // CORES, CORES, tile_count), ("side", "core", "tile"))
    split = ("side", "core", "tile")
    return jax.shard_map(
        per_device,
        mesh=fine,
        in_specs=(P(split, None, None, None, None), P(split, None, None, None, None), P(split, None)),
        out_specs=P("tile", ("side", "core"), None),
        check_vma=False,
    )
```

time: 143 us -> 72 us (0.50)
  waiting for transfers between devices: 71.5 us -> 42.5 us
  blocking collectives: 19.9 us -> 0 us
  between operations: 14.2 us -> 0.09 us
  Pallas kernels: 0 us -> 8.16 us
  matrix products: 5.91 us -> 0 us
  starting transfers between devices: 20.6 us -> 14.8 us
  local copies, waits for them, and re-layouts: 8.1 us -> 3.05 us
    unnamed x2 -> x0, waiting for transfers between devices: 51.9 us -> none
    all_gather x1 -> x0, blocking collectives: 19.9 us -> none  [per_device(): corner_all = lax.all_gather(corners, 'tile', axis=0, tiled=True)]
    ppermute x4, waiting for transfers between devices: 6.73 us -> 18.4 us  [the longest x1 13.6 us: per_device(): lax.ppermute(parts[step], 'side', [(i, (i + step) % sides) for i in range...]
    all_to_all x2 -> x1, waiting for transfers between devices: 12.9 us -> 24.1 us  [per_device(): lax.all_to_all(packed, ('tile', 'core'), split_axis=0, concat_axis=0, til...]
    pallas_call x0 -> x3, Pallas kernels: none -> 8.16 us  [the longest x1 4.12 us: per_device(): pl.pallas_call(functools.partial(place_kernel, (shots, times, planes, row...]
    dot_general x2 -> x0, matrix products: 5.91 us -> none  [the longest x1 3.63 us: per_device(): jnp.einsum('rx,qzry->qzxy', row_table, placed, precision=lax.Precision.HI...]
    all_to_all x2 -> x1, starting transfers between devices: 10.3 us -> 6.63 us  [per_device(): lax.all_to_all(packed, ('tile', 'core'), split_axis=0, concat_axis=0, til...]
    squeeze x3 -> x0, local copies, waits for them, and re-layouts: 2.87 us -> none  [the longest x2 1.56 us: per_device(): image_part = sums[0]]
  transfers between devices with their start and end apart: 7 -> 5, of which waited for: 4 -> 3; matrix products, arithmetic and copies ran while one was open for 1% -> 1% of each run, Pallas kernels for 0% -> 0%
where the time goes in v1:
time: 72 us; the launch traced here: 71.7 us
  waiting for transfers between devices  42.5 us (59%)
  starting transfers between devices  14.8 us (21%)
  Pallas kernels  8.16 us (11%)
  other arithmetic  3.12 us (4%)
  local copies, waits for them, and re-layouts  3.05 us (4%)
    all_to_all x1, waiting for transfers between devices, per_device(): lax.all_to_all(packed, ('tile', 'core'), split_axis=0, concat_axis=0, til...  24.1 us
    ppermute x1, waiting for transfers between devices, per_device(): lax.ppermute(parts[step], 'side', [(i, (i + step) % sides) for i in range...  13.6 us
    all_to_all x1, starting transfers between devices, per_device(): lax.all_to_all(packed, ('tile', 'core'), split_axis=0, concat_axis=0, til...  6.63 us
    ppermute x1, waiting for transfers between devices, per_device(): across = lax.ppermute(across, names, cross)  4.75 us
    ppermute x1, starting transfers between devices, per_device(): straight = lax.ppermute(straight, names, along)  4.57 us
    pallas_call x1, Pallas kernels, per_device(): pl.pallas_call(functools.partial(place_kernel, (shots, times, planes, row...  4.12 us
    pallas_call x1, Pallas kernels, per_device(): pl.pallas_call(functools.partial(normal_kernel, (planes, half, sides)), o...  2.06 us
    pallas_call x1, Pallas kernels, per_device(): pl.pallas_call(functools.partial(laplace_kernel, (planes, strip)), out_sh...  1.98 us
  transfers between devices with their start and end apart: 5, of which 3 were waited for; matrix products, arithmetic and copies ran while one was open for 1% of the time, Pallas kernels for 0%

profile of v1, /device:TPU:3, one launch (start us, length us, event | category | flops | bytes accessed | tf_op | source)
XLA Modules:
  0.0 71.7 jit_solution(18217000290698089384)
XLA Ops:
  0.0 0.0 copy-start.2
  0.0 0.7 %convert_element_type.10 = bf16[2,2]{1,0:T(2,128)(2,1)S(1)} convert(s32[2,2]{1,0:T(2,128)} %param.5) | non-fusion elementwise | flops 4 | bytes 24 | tf_op jit(solution)/shard_map/convert_element_type | solution.py:159
  0.7 0.1 reshape.22
  0.8 1.1 %copy.8 = bf16[2,1,16,2,32,128]{5,4,3,0,2,1:T(8,128)(2,1)S(1)} copy(bf16[2,1,16,2,32,128]{5,4,3,2,0,1:T(8,128)(2,1)} %bitcast.13) | data formatting | bytes 1048576 | tf_op jit(solution)/shard_map/reshape | solution.py:156
  1.9 0.0 copy-done.2
  2.0 1.1 %pad_maximum_fusion = bf16[16,272,128]{2,1,0:T(8,128)(2,1)} fusion(bf16[16,16,128]{2,1,0:T(8,128)(2,1)S(1)} %broadcast_in_dim.2, bf16[16,128,128]{2,1,0:T(8,128)(2,1)S(1)} %bitcast.12, bf16[16,128,128]{2,1,0:T(8,128)(2,1)S(1)} %bitcast.11), kind=kLoop, calls=%fused_computation | loop fusion | flops 3342336 | bytes 2228224 | tf_op jit(solution)/shard_map/concatenate | solution.py:161
  3.1 6.6 %all-to-all-start = ((bf16[16,272,128]{2,1,0:T(8,128)(2,1)}), bf16[16,272,128]{2,1,0:T(8,128)(2,1)S(1)}, u32[]{:S(2)}, u32[]{:S(2)}) async-start(bf16[16,272,128]{2,1,0:T(8,128)(2,1)} %pad_maximum_fusion), calls=%async_computation | async-start | bytes 2228224 | tf_op jit(solution)/shard_map/all_to_all | solution.py:162
  9.7 0.6 pad_add_fusion.spot_ref
  10.4 24.1 %all-to-all-done.got_ref = bf16[16,272,128]{2,1,0:T(8,128)(2,1)S(1)} async-done(((bf16[16,272,128]{2,1,0:T(8,128)(2,1)}), bf16[16,272,128]{2,1,0:T(8,128)(2,1)S(1)}, u32[]{:S(2)}, u32[]{:S(2)}) %all-to-all-start) | async-done | bytes 1114144 | tf_op jit(solution)/shard_map/all_to_all | solution.py:162
  34.5 0.0 copy-start
  34.5 0.6 slice_convert_fusion
  35.1 0.4 copy-done
  35.5 4.1 %shard_map.37 = (f32[2,2,136,256]{3,2,1,0:T(8,128)}, f32[2,2,136,256]{3,2,1,0:T(8,128)}) custom-call(s32[16,4]{1,0:T(8,128)} %bitcast.15, s32[2]{0:T(128)} %pad_add_fusion.spot_ref, bf16[16,272,128]{2,1,0:T(8,128)(2,1)} %copy-done), custom_call_target="tpu_custom_call" | custom-call | tf_op jit(solution)/shard_map/pallas_call | solution.py:167
  39.6 1.2 %collective-permute-start = (f32[2,2,136,256]{3,2,1,0:T(8,128)}, f32[2,2,136,256]{3,2,1,0:T(8,128)S(1)}, u32[]{:S(2)}, u32[]{:S(2)}) collective-permute-start(f32[2,2,136,256]{3,2,1,0:T(8,128)} %get-tuple-element.12), channel_id=1, source_target_pairs={{0,16},{16,0},{1,17},{17,1},{2,18},{18,2},{3,19},{19,3},{4,20},{20... | collective-permute-start | bytes 1671176 | tf_op jit(solution)/shard_map/ppermute | solution.py:175
  40.8 13.6 %collective-permute-done.refs_1_ = f32[2,2,136,256]{3,2,1,0:T(8,128)S(1)} collective-permute-done((f32[2,2,136,256]{3,2,1,0:T(8,128)}, f32[2,2,136,256]{3,2,1,0:T(8,128)S(1)}, u32[]{:S(2)}, u32[]{:S(2)}) %collective-permute-start) | collective-permute-done | bytes 557088 | tf_op jit(solution)/shard_map/ppermute | solution.py:175
  54.5 0.0 copy-start.1
  54.5 0.8 %copy-done.1 = f32[2,2,136,256]{3,2,1,0:T(8,128)} copy-done((f32[2,2,136,256]{3,2,1,0:T(8,128)}, f32[2,2,136,256]{3,2,1,0:T(8,128)S(1)}, u32[]{:S(2)}) %copy-start.1) | copy-done | bytes 557080
  55.3 2.1 %shard_map.38 = (f32[2,72,256]{2,1,0:T(8,128)}, f32[2,72,256]{2,1,0:T(8,128)}, f32[64,256]{1,0:T(8,128)}, f32[64,256]{1,0:T(8,128)}) custom-call(s32[2]{0:T(128)} %pad_add_fusion.spot_ref, f32[2,2,136,256]{3,2,1,0:T(8,128)} %get-tuple-element.11.refs_0_, f32[2,2,136,256]{3,2,1,0:T(8,128)} %copy-done.1), custom_call_target="tpu_custom_call" | custom-call | tf_op jit(solution)/shard_map/pallas_call | solution.py:181
  57.3 0.4 collective-permute-start.1
  57.7 4.6 %collective-permute-start.2 = (f32[64,256]{1,0:T(8,128)}, f32[64,256]{1,0:T(8,128)S(1)}, u32[]{:S(2)}, u32[]{:S(2)}) collective-permute-start(f32[64,256]{1,0:T(8,128)} %get-tuple-element.15), channel_id=1, source_target_pairs={{1,0},{2,1},{3,2},{4,3},{5,4},{6,5},{7,6},{8,9},{9,10},{10,11},{11... | collective-permute-start | bytes 196616 | tf_op jit(solution)/shard_map/ppermute | solution.py:195
  62.3 1.9 %collective-permute-start.3 = (f32[64,256]{1,0:T(8,128)}, f32[64,256]{1,0:T(8,128)S(1)}, u32[]{:S(2)}, u32[]{:S(2)}) collective-permute-start(f32[64,256]{1,0:T(8,128)} %get-tuple-element.16), channel_id=1, source_target_pairs={{1,8},{2,9},{3,10},{4,11},{5,12},{6,13},{7,14},{8,1},{9,2},{10,3},... | collective-permute-start | bytes 196616 | tf_op jit(solution)/shard_map/ppermute | solution.py:196
  64.2 0.0 collective-permute-done.2.straight
  64.2 0.0 copy-start.4
  64.2 4.7 %collective-permute-done.3.across = f32[64,256]{1,0:T(8,128)S(1)} collective-permute-done((f32[64,256]{1,0:T(8,128)}, f32[64,256]{1,0:T(8,128)S(1)}, u32[]{:S(2)}, u32[]{:S(2)}) %collective-permute-start.3) | collective-permute-done | bytes 65568 | tf_op jit(solution)/shard_map/ppermute | solution.py:196
  69.0 0.0 copy-start.5
  69.0 0.0 collective-permute-done.1.got
  69.0 0.0 copy-start.3
  69.0 0.0 copy-done.4
  69.0 0.6 copy-done.5
  69.6 0.1 copy-done.3
  69.7 2.0 %shard_map.39 = f32[4,64,256]{2,1,0:T(8,128)} custom-call(s32[2]{0:T(128)} %pad_add_fusion.spot_ref, f32[2,72,256]{2,1,0:T(8,128)} %get-tuple-element.13.keep, f32[2,72,256]{2,1,0:T(8,128)} %copy-done.3, f32[64,256]{1,0:T(8,128)} %copy-done.4, f32[64,256]{1,0:T(8,128)} %copy-done.5), custom_call_target="tpu_custom_call" | custom-call | tf_op jit(solution)/shard_map/pallas_call | solution.py:198
  (3 shorter events, 0.1 us)
Async XLA Ops:
  0.0 1.9 %copy-start.2 = (bf16[2,1,32,32,128]{4,3,2,1,0:T(8,128)(2,1)S(1)}, bf16[2,1,32,32,128]{4,3,2,1,0:T(8,128)(2,1)}, u32[]{:S(2)}) copy-start(bf16[2,1,32,32,128]{4,3,2,1,0:T(8,128)(2,1)} %param.4) | copy-start | bytes 1572868
  3.1 31.4 %all-to-all-start = ((bf16[16,272,128]{2,1,0:T(8,128)(2,1)}), bf16[16,272,128]{2,1,0:T(8,128)(2,1)S(1)}, u32[]{:S(2)}, u32[]{:S(2)}) async-start(bf16[16,272,128]{2,1,0:T(8,128)(2,1)} %pad_maximum_fusion), calls=%async_computation | async-start | bytes 2228224 | tf_op jit(solution)/shard_map/all_to_all | solution.py:162
  34.5 1.0 %copy-start = (bf16[16,272,128]{2,1,0:T(8,128)(2,1)}, bf16[16,272,128]{2,1,0:T(8,128)(2,1)S(1)}, u32[]{:S(2)}) copy-start(bf16[16,272,128]{2,1,0:T(8,128)(2,1)S(1)} %all-to-all-done.got_ref) | copy-start | bytes 3342340
  39.6 14.9 %collective-permute-start = (f32[2,2,136,256]{3,2,1,0:T(8,128)}, f32[2,2,136,256]{3,2,1,0:T(8,128)S(1)}, u32[]{:S(2)}, u32[]{:S(2)}) collective-permute-start(f32[2,2,136,256]{3,2,1,0:T(8,128)} %get-tuple-element.12), channel_id=1, source_target_pairs={{0,16},{16,0},{1,17},{17,1},{2,18},{18,2},{3,19},{19,3},{4,20},{20... | collective-permute-start | bytes 1671176 | tf_op jit(solution)/shard_map/ppermute | solution.py:175
  54.5 0.8 %copy-start.1 = (f32[2,2,136,256]{3,2,1,0:T(8,128)}, f32[2,2,136,256]{3,2,1,0:T(8,128)S(1)}, u32[]{:S(2)}) copy-start(f32[2,2,136,256]{3,2,1,0:T(8,128)S(1)} %collective-permute-done.refs_1_) | copy-start | bytes 1671172
  57.3 11.7 %collective-permute-start.1 = (f32[2,72,256]{2,1,0:T(8,128)}, f32[2,72,256]{2,1,0:T(8,128)S(1)}, u32[]{:S(2)}, u32[]{:S(2)}) collective-permute-start(f32[2,72,256]{2,1,0:T(8,128)} %get-tuple-element.14), channel_id=1, source_target_pairs={{0,8},{1,9},{2,10},{3,11},{4,12},{5,13},{6,14},{7,15},{8,0},{9,1},... | collective-permute-start | bytes 442376 | tf_op jit(solution)/shard_map/ppermute | solution.py:197
  57.7 6.5 %collective-permute-start.2 = (f32[64,256]{1,0:T(8,128)}, f32[64,256]{1,0:T(8,128)S(1)}, u32[]{:S(2)}, u32[]{:S(2)}) collective-permute-start(f32[64,256]{1,0:T(8,128)} %get-tuple-element.15), channel_id=1, source_target_pairs={{1,0},{2,1},{3,2},{4,3},{5,4},{6,5},{7,6},{8,9},{9,10},{10,11},{11... | collective-permute-start | bytes 196616 | tf_op jit(solution)/shard_map/ppermute | solution.py:195
  62.3 6.7 %collective-permute-start.3 = (f32[64,256]{1,0:T(8,128)}, f32[64,256]{1,0:T(8,128)S(1)}, u32[]{:S(2)}, u32[]{:S(2)}) collective-permute-start(f32[64,256]{1,0:T(8,128)} %get-tuple-element.16), channel_id=1, source_target_pairs={{1,8},{2,9},{3,10},{4,11},{5,12},{6,13},{7,14},{8,1},{9,2},{10,3},... | collective-permute-start | bytes 196616 | tf_op jit(solution)/shard_map/ppermute | solution.py:196
  64.2 4.8 %copy-start.4 = (f32[64,256]{1,0:T(8,128)}, f32[64,256]{1,0:T(8,128)S(1)}, u32[]{:S(2)}) copy-start(f32[64,256]{1,0:T(8,128)S(1)} %collective-permute-done.2.straight) | copy-start | bytes 196612
  69.0 0.6 copy-start.5
  69.0 0.7 copy-start.3

commit v2 on v1

--- a/solution.py
+++ b/solution.py
@@ -12,6 +12,7 @@
 LANES = 128
 CORES = 2
 EDGE = 8
+GRANT = 12 << 20
 
 damping = 1.0
 
@@ -169,6 +170,7 @@
         out_shape=[part_shape] * sides,
         in_specs=[smem, smem] + whole(1),
         out_specs=whole(sides),
+        compiler_params=pltpu.CompilerParams(vmem_limit_bytes=GRANT),
         scratch_shapes=[pltpu.VMEM((Y // LANES, 2, planes, X, LANES), jnp.float32)],
     )(corner_all, spot, got)
     parts = [parts[0]] + [
@@ -183,6 +185,7 @@
         out_shape=[strip_shape, strip_shape, plane_shape, plane_shape],
         in_specs=[smem] + whole(sides),
         out_specs=whole(4),
+        compiler_params=pltpu.CompilerParams(vmem_limit_bytes=GRANT),
         scratch_shapes=[pltpu.VMEM((planes, half + EDGE, Y), jnp.float32)],
     )(spot, *parts)
     at = lambda c, t: c * tiles + t
@@ -200,6 +203,7 @@
         out_shape=jax.ShapeDtypeStruct((planes * CORES, strip, Y), jnp.float32),
         in_specs=[smem] + whole(4),
         out_specs=pl.BlockSpec(memory_space=pltpu.VMEM),
+        compiler_params=pltpu.CompilerParams(vmem_limit_bytes=GRANT),
     )(spot, keep, got_strip, straight, across)
 
 

time: 72 us -> 65.7 us (0.913)
  Pallas kernels: 8.16 us -> 4.71 us
  local copies, waits for them, and re-layouts: 3.05 us -> 1.22 us
  other arithmetic: 3.12 us -> 1.9 us
    unnamed x12 -> x2, local copies, waits for them, and re-layouts: 1.84 us -> 0.01 us
    pallas_call x1, Pallas kernels: 4.12 us -> 2.54 us  [per_device(): pl.pallas_call(functools.partial(place_kernel, (shots, times, planes, row...]
    pallas_call x1, Pallas kernels: 2.06 us -> 0.66 us  [per_device(): pl.pallas_call(functools.partial(normal_kernel, (planes, half, sides)), o...]
  transfers between devices with their start and end apart: 5 -> 5, of which waited for: 3 -> 3; matrix products, arithmetic and copies ran while one was open for 1% -> 0% of each run, Pallas kernels for 0% -> 0%
where the time goes in v2:
time: 65.7 us; the launch traced here: 65.4 us
  waiting for transfers between devices  42.6 us (65%)
  starting transfers between devices  14.9 us (23%)
  Pallas kernels  4.71 us (7%)
  other arithmetic  1.9 us (3%)
  local copies, waits for them, and re-layouts  1.22 us (2%)
    all_to_all x1, waiting for transfers between devices, per_device(): lax.all_to_all(packed, ('tile', 'core'), split_axis=0, concat_axis=0, til...  24.7 us
    ppermute x1, waiting for transfers between devices, per_device(): lax.ppermute(parts[step], 'side', [(i, (i + step) % sides) for i in range...  13.4 us
    all_to_all x1, starting transfers between devices, per_device(): lax.all_to_all(packed, ('tile', 'core'), split_axis=0, concat_axis=0, til...  6.63 us
    ppermute x1, starting transfers between devices, per_device(): straight = lax.ppermute(straight, names, along)  4.57 us
    ppermute x1, waiting for transfers between devices, per_device(): across = lax.ppermute(across, names, cross)  4.54 us
    pallas_call x1, Pallas kernels, per_device(): pl.pallas_call(functools.partial(place_kernel, (shots, times, planes, row...  2.54 us
    ppermute x1, starting transfers between devices, per_device(): across = lax.ppermute(across, names, cross)  1.92 us
    pallas_call x1, Pallas kernels, per_device(): pl.pallas_call(functools.partial(laplace_kernel, (planes, strip)), out_sh...  1.51 us
  transfers between devices with their start and end apart: 5, of which 3 were waited for; matrix products, arithmetic and copies ran while one was open for 0% of the time, Pallas kernels for 0%

profile of v2, /device:TPU:3, one launch (start us, length us, event | category | flops | bytes accessed | tf_op | source)
XLA Modules:
  0.0 65.4 jit_solution(8406208955561892712)
XLA Ops:
  0.0 0.0 copy-start
  0.0 0.7 %convert_element_type.10 = bf16[2,2]{1,0:T(2,128)(2,1)S(1)} convert(s32[2,2]{1,0:T(2,128)} %param.5) | non-fusion elementwise | flops 4 | bytes 24 | tf_op jit(solution)/shard_map/convert_element_type | solution.py:160
  0.7 0.1 reshape.22
  0.8 1.1 %copy.8 = bf16[2,1,16,2,32,128]{5,4,3,0,2,1:T(8,128)(2,1)S(1)} copy(bf16[2,1,16,2,32,128]{5,4,3,2,0,1:T(8,128)(2,1)} %bitcast.14) | data formatting | bytes 1048576 | tf_op jit(solution)/shard_map/reshape | solution.py:157
  1.9 0.0 copy-done
  2.0 1.1 %pad_maximum_fusion = bf16[16,272,128]{2,1,0:T(8,128)(2,1)} fusion(bf16[16,16,128]{2,1,0:T(8,128)(2,1)S(1)} %broadcast_in_dim.2, bf16[16,128,128]{2,1,0:T(8,128)(2,1)S(1)} %bitcast.13, bf16[16,128,128]{2,1,0:T(8,128)(2,1)S(1)} %bitcast.12), kind=kLoop, calls=%fused_computation | loop fusion | flops 3342336 | bytes 2228224 | tf_op jit(solution)/shard_map/concatenate | solution.py:162
  3.1 6.6 %all-to-all-start = ((bf16[16,272,128]{2,1,0:T(8,128)(2,1)}), bf16[16,272,128]{2,1,0:T(8,128)(2,1)S(1)}, u32[]{:S(2)}, u32[]{:S(2)}) async-start(bf16[16,272,128]{2,1,0:T(8,128)(2,1)} %pad_maximum_fusion), calls=%async_computation | async-start | bytes 2228224 | tf_op jit(solution)/shard_map/all_to_all | solution.py:163
  9.7 0.1 pad_add_fusion.spot_ref
  9.8 24.7 %all-to-all-done.got_ref = bf16[16,272,128]{2,1,0:T(8,128)(2,1)S(1)} async-done(((bf16[16,272,128]{2,1,0:T(8,128)(2,1)}), bf16[16,272,128]{2,1,0:T(8,128)(2,1)S(1)}, u32[]{:S(2)}, u32[]{:S(2)}) %all-to-all-start) | async-done | bytes 1114144 | tf_op jit(solution)/shard_map/all_to_all | solution.py:163
  34.5 2.5 %shard_map.37 = (f32[2,2,136,256]{3,2,1,0:T(8,128)S(1)}, f32[2,2,136,256]{3,2,1,0:T(8,128)S(1)}) custom-call(s32[16,4]{1,0:T(8,128)S(1)} %bitcast.11, s32[2]{0:T(128)S(1)} %pad_add_fusion.spot_ref, bf16[16,272,128]{2,1,0:T(8,128)(2,1)S(1)} %all-to-all-done.got_ref), custom_call_target="tpu_custom_call" | custom-call | tf_op jit(solution)/shard_map/pallas_call | solution.py:168
  37.0 1.3 %collective-permute-start = (f32[2,2,136,256]{3,2,1,0:T(8,128)S(1)}, f32[2,2,136,256]{3,2,1,0:T(8,128)S(1)}, u32[]{:S(2)}, u32[]{:S(2)}) collective-permute-start(f32[2,2,136,256]{3,2,1,0:T(8,128)S(1)} %get-tuple-element.12), channel_id=1, source_target_pairs={{0,16},{16,0},{1,17},{17,1},{2,18},{18,2},{3,19},{19,3},{4,20},{20... | collective-permute-start | bytes 1671176 | tf_op jit(solution)/shard_map/ppermute | solution.py:177
  38.3 13.4 %collective-permute-done.refs_1_ = f32[2,2,136,256]{3,2,1,0:T(8,128)S(1)} collective-permute-done((f32[2,2,136,256]{3,2,1,0:T(8,128)S(1)}, f32[2,2,136,256]{3,2,1,0:T(8,128)S(1)}, u32[]{:S(2)}, u32[]{:S(2)}) %collective-permute-start) | collective-permute-done | bytes 557088 | tf_op jit(solution)/shard_map/ppermute | solution.py:177
  51.7 0.7 %shard_map.38 = (f32[2,72,256]{2,1,0:T(8,128)S(1)}, f32[2,72,256]{2,1,0:T(8,128)S(1)}, f32[64,256]{1,0:T(8,128)S(1)}, f32[64,256]{1,0:T(8,128)S(1)}) custom-call(s32[2]{0:T(128)S(1)} %pad_add_fusion.spot_ref, f32[2,2,136,256]{3,2,1,0:T(8,128)S(1)} %get-tuple-element.11.refs_0_, f32[2,2,136,256]{3,2,1,0:T(8,128)S(1)} %collective-permute-done.refs_1_), custom_call_target="tpu_custom_call" | custom-call | tf_op jit(solution)/shard_map/pallas_call | solution.py:183
  52.4 0.5 collective-permute-start.1
  52.9 4.6 %collective-permute-start.2 = (f32[64,256]{1,0:T(8,128)S(1)}, f32[64,256]{1,0:T(8,128)S(1)}, u32[]{:S(2)}, u32[]{:S(2)}) collective-permute-start(f32[64,256]{1,0:T(8,128)S(1)} %get-tuple-element.15), channel_id=1, source_target_pairs={{1,0},{2,1},{3,2},{4,3},{5,4},{6,5},{7,6},{8,9},{9,10},{10,11},{11... | collective-permute-start | bytes 196616 | tf_op jit(solution)/shard_map/ppermute | solution.py:198
  57.4 1.9 %collective-permute-start.3 = (f32[64,256]{1,0:T(8,128)S(1)}, f32[64,256]{1,0:T(8,128)S(1)}, u32[]{:S(2)}, u32[]{:S(2)}) collective-permute-start(f32[64,256]{1,0:T(8,128)S(1)} %get-tuple-element.16), channel_id=1, source_target_pairs={{1,8},{2,9},{3,10},{4,11},{5,12},{6,13},{7,14},{8,1},{9,2},{10,3},... | collective-permute-start | bytes 196616 | tf_op jit(solution)/shard_map/ppermute | solution.py:199
  59.4 0.0 collective-permute-done.2.straight
  59.4 4.5 %collective-permute-done.3.across = f32[64,256]{1,0:T(8,128)S(1)} collective-permute-done((f32[64,256]{1,0:T(8,128)S(1)}, f32[64,256]{1,0:T(8,128)S(1)}, u32[]{:S(2)}, u32[]{:S(2)}) %collective-permute-start.3) | collective-permute-done | bytes 65568 | tf_op jit(solution)/shard_map/ppermute | solution.py:199
  63.9 0.0 collective-permute-done.1.got
  63.9 1.5 %shard_map.39 = f32[4,64,256]{2,1,0:T(8,128)} custom-call(s32[2]{0:T(128)S(1)} %pad_add_fusion.spot_ref, f32[2,72,256]{2,1,0:T(8,128)S(1)} %get-tuple-element.13.keep, f32[2,72,256]{2,1,0:T(8,128)S(1)} %collective-permute-done.1.got, f32[64,256]{1,0:T(8,128)S(1)} %collective-permute-done.2.straight, f32[64,256]{1,0:T(8,128)S(1)} %collective-permute-done.3.across), custom_call_target="tpu_custom_call" | custom-call | tf_op jit(solution)/shard_map/pallas_call | solution.py:201
  (4 shorter events, 0.1 us)
Async XLA Ops:
  0.0 1.9 %copy-start = (bf16[2,1,32,32,128]{4,3,2,1,0:T(8,128)(2,1)S(1)}, bf16[2,1,32,32,128]{4,3,2,1,0:T(8,128)(2,1)}, u32[]{:S(2)}) copy-start(bf16[2,1,32,32,128]{4,3,2,1,0:T(8,128)(2,1)} %param.4) | copy-start | bytes 1572868
  3.1 31.4 %all-to-all-start = ((bf16[16,272,128]{2,1,0:T(8,128)(2,1)}), bf16[16,272,128]{2,1,0:T(8,128)(2,1)S(1)}, u32[]{:S(2)}, u32[]{:S(2)}) async-start(bf16[16,272,128]{2,1,0:T(8,128)(2,1)} %pad_maximum_fusion), calls=%async_computation | async-start | bytes 2228224 | tf_op jit(solution)/shard_map/all_to_all | solution.py:163
  37.0 14.7 %collective-permute-start = (f32[2,2,136,256]{3,2,1,0:T(8,128)S(1)}, f32[2,2,136,256]{3,2,1,0:T(8,128)S(1)}, u32[]{:S(2)}, u32[]{:S(2)}) collective-permute-start(f32[2,2,136,256]{3,2,1,0:T(8,128)S(1)} %get-tuple-element.12), channel_id=1, source_target_pairs={{0,16},{16,0},{1,17},{17,1},{2,18},{18,2},{3,19},{19,3},{4,20},{20... | collective-permute-start | bytes 1671176 | tf_op jit(solution)/shard_map/ppermute | solution.py:177
  52.4 11.5 %collective-permute-start.1 = (f32[2,72,256]{2,1,0:T(8,128)S(1)}, f32[2,72,256]{2,1,0:T(8,128)S(1)}, u32[]{:S(2)}, u32[]{:S(2)}) collective-permute-start(f32[2,72,256]{2,1,0:T(8,128)S(1)} %get-tuple-element.14), channel_id=1, source_target_pairs={{0,8},{1,9},{2,10},{3,11},{4,12},{5,13},{6,14},{7,15},{8,0},{9,1},... | collective-permute-start | bytes 442376 | tf_op jit(solution)/shard_map/ppermute | solution.py:200
  52.9 6.5 %collective-permute-start.2 = (f32[64,256]{1,0:T(8,128)S(1)}, f32[64,256]{1,0:T(8,128)S(1)}, u32[]{:S(2)}, u32[]{:S(2)}) collective-permute-start(f32[64,256]{1,0:T(8,128)S(1)} %get-tuple-element.15), channel_id=1, source_target_pairs={{1,0},{2,1},{3,2},{4,3},{5,4},{6,5},{7,6},{8,9},{9,10},{10,11},{11... | collective-permute-start | bytes 196616 | tf_op jit(solution)/shard_map/ppermute | solution.py:198
  57.4 6.5 %collective-permute-start.3 = (f32[64,256]{1,0:T(8,128)S(1)}, f32[64,256]{1,0:T(8,128)S(1)}, u32[]{:S(2)}, u32[]{:S(2)}) collective-permute-start(f32[64,256]{1,0:T(8,128)S(1)} %get-tuple-element.16), channel_id=1, source_target_pairs={{1,8},{2,9},{3,10},{4,11},{5,12},{6,13},{7,14},{8,1},{9,2},{10,3},... | collective-permute-start | bytes 196616 | tf_op jit(solution)/shard_map/ppermute | solution.py:199

commit v3 on v1

v3 whole, which is shorter than its diff:
```python
import functools

import jax
import jax.numpy as jnp
from jax import lax
from jax.experimental import pallas as pl
from jax.experimental.pallas import tpu as pltpu
from jax.sharding import Mesh, PartitionSpec as P

X = 256
Y = 256
LANES = 128
CORES = 2
EDGE = 8
GRANT = 12 << 20
COVER = 10 ** 7

damping = 1.0


def whole(count):
    return [pl.BlockSpec(memory_space=pltpu.VMEM)] * count


def place_kernel(dims, corner_ref, spot_ref, got_ref, *refs):
    shots, times, planes, rows, sides, half = dims
    outs, total = refs[:-1], refs[-1]
    senders = got_ref.shape[0]
    field = shots * times * planes * rows
    total[...] = jnp.zeros_like(total)
    lane = lax.broadcasted_iota(jnp.int32, (rows, LANES), 1)

    def one_sender(sender, carry):
        for shot in range(shots):
            row = corner_ref[sender, 2 * shot]
            col = corner_ref[sender, 2 * shot + 1]
            turn = lax.rem(col, LANES)
            first = lane >= col
            sums = []
            for plane in range(planes):
                image = light = None
                for time in range(times):
                    at = ((shot * times + time) * planes + plane) * rows
                    wave = got_ref[sender, at:at + rows, :].astype(jnp.float32)
                    back = got_ref[sender, field + at:field + at + rows, :].astype(jnp.float32)
                    image = wave * back if image is None else image + wave * back
                    light = wave * wave if light is None else light + wave * wave
                sums.append((0, plane, pltpu.roll(image, turn, 1)))
                sums.append((1, plane, pltpu.roll(light, turn, 1)))
            span = pl.ds(row, rows)
            fresh = []
            for kind, plane, value in sums:
                low = total[0, kind, plane, span, :]
                high = total[1, kind, plane, span, :]
                fresh.append((kind, plane, low + jnp.where(first, value, 0.0), high + jnp.where(first, 0.0, value)))
            for kind, plane, low, high in fresh:
                total[0, kind, plane, span, :] = low
                total[1, kind, plane, span, :] = high
        return carry

    lax.fori_loop(0, senders, one_sender, 0)
    side = spot_ref[0]
    core = spot_ref[1]
    strip = half // CORES
    slot = lax.broadcasted_iota(jnp.int32, (EDGE, LANES), 0)
    for step, out in enumerate(outs):
        target = lax.rem(side + step // CORES, sides) * CORES + lax.rem(core + step % CORES, CORES)
        start = pl.multiple_of(target * strip, strip)
        before = pl.multiple_of(lax.max(start - EDGE, 0), EDGE)
        after = pl.multiple_of(lax.min(start + strip, X - EDGE), EDGE)
        for kind in range(2):
            for plane in range(planes):
                for tile in range(Y // LANES):
                    lanes = slice(tile * LANES, (tile + 1) * LANES)
                    out[kind, plane, :strip, lanes] = total[tile, kind, plane, pl.ds(start, strip), :]
                    above = total[tile, kind, plane, pl.ds(before, EDGE), :]
                    below = total[tile, kind, plane, pl.ds(after, EDGE), :]
                    above = jnp.where(target > 0, above, 0.0)
                    below = jnp.where(target < sides * CORES - 1, below, 0.0)
                    pair = jnp.where(slot == EDGE - 1, above, jnp.where(slot == 0, below, 0.0))
                    out[kind, plane, strip:, lanes] = pair


def pack_kernel(corner_ref, source, receiver, out, sems):
    shots, times, spread, planes, rows, cols = source.shape
    cell = planes * rows
    copies = []
    for kind, field in enumerate((source, receiver)):
        for shot in range(shots):
            for time in range(times):
                block = (kind * shots + shot) * times + time
                for plane in range(planes):
                    at = block * cell + plane * rows
                    copy = pltpu.make_async_copy(
                        field.at[shot, time, :, plane], out.at[:, at:at + rows, :], sems.at[block * planes + plane]
                    )
                    copy.start()
                    copies.append(copy)
    lane = lax.broadcasted_iota(jnp.int32, (2 * EDGE, cols), 1)
    tag = jnp.zeros((2 * EDGE, cols), jnp.float32)
    for shot in range(shots):
        for which in range(2):
            tag = jnp.where(lane == 2 * shot + which, corner_ref[shot, which].astype(jnp.float32), tag)
    tag = tag.astype(jnp.bfloat16)
    end = 2 * shots * times * cell
    for target in range(spread):
        out[target, end:, :] = tag
    for copy in copies:
        copy.wait()


def normal_kernel(dims, spot_ref, *refs):
    planes, strip, parts = dims
    ins, (cells, low, high) = refs[:parts], refs[parts:]
    core = spot_ref[1]
    for turn in range(CORES):
        base = lax.rem(core + turn, CORES) * planes
        image = ins[turn][0]
        light = ins[turn][1]
        for part in ins[turn + CORES::CORES]:
            image = image + part[0]
            light = light + part[1]
        normal = image / (damping + light)
        for plane in range(planes):
            cells[base + plane] = normal[plane]
    low[...] = cells[0, :strip, :]
    high[...] = cells[planes * CORES - 1, :strip, :]


def lateral_kernel(dims, cells, out):
    depth, strip = dims
    row = lax.broadcasted_iota(jnp.int32, (strip, Y), 0)
    col = lax.broadcasted_iota(jnp.int32, (strip, Y), 1)
    for plane in range(depth):
        body = cells[plane, :strip, :]
        above = jnp.where(row == 0, cells[plane, strip + EDGE - 1:, :], pltpu.roll(body, 1, 0))
        below = jnp.where(row == strip - 1, cells[plane, strip:strip + 1, :], pltpu.roll(body, strip - 1, 0))
        left = jnp.where(col == 0, 0.0, pltpu.roll(body, 1, 1))
        right = jnp.where(col == Y - 1, 0.0, pltpu.roll(body, Y - 1, 1))
        value = above + below + left + right - 6.0 * body
        if plane > 0:
            value = value + cells[plane - 1, :strip, :]
        if plane < depth - 1:
            value = value + cells[plane + 1, :strip, :]
        out[plane] = value


def faces_kernel(inner, under, over, out):
    depth = inner.shape[0]
    for plane in range(depth):
        value = inner[plane]
        if plane == 0:
            value = value + under[...]
        if plane == depth - 1:
            value = value + over[...]
        out[plane] = value


def per_device(source, receiver, corners):
    sides = lax.axis_size("side")
    tiles = lax.axis_size("tile")
    spread = tiles * CORES
    shots, times, depth, rows, cols = source.shape
    planes = depth // spread
    half = X // sides
    strip = half // CORES
    side = lax.axis_index("side")
    core = lax.axis_index("core")
    spot = jnp.stack([side, core]).astype(jnp.int32)
    smem = pl.BlockSpec(memory_space=pltpu.SMEM)
    params = pltpu.CompilerParams(vmem_limit_bytes=GRANT)

    blocks = 2 * shots * times * planes
    raw = [field.reshape(shots, times, spread, planes, rows, cols) for field in (source, receiver)]
    packed = pl.pallas_call(
        pack_kernel,
        out_shape=jax.ShapeDtypeStruct((spread, blocks * rows + 2 * EDGE, cols), jnp.bfloat16),
        in_specs=[smem] + [pl.BlockSpec(memory_space=pltpu.HBM)] * 2,
        out_specs=pl.BlockSpec(memory_space=pltpu.VMEM),
        scratch_shapes=[pltpu.SemaphoreType.DMA((blocks,))],
        compiler_params=params,
    )(corners, *raw)
    got = lax.all_to_all(packed, ("tile", "core"), split_axis=0, concat_axis=0, tiled=True)
    corner_all = got[:, -2 * EDGE, : 2 * shots].astype(jnp.int32)

    group = sides * CORES
    parts = pl.pallas_call(
        functools.partial(place_kernel, (shots, times, planes, rows, sides, half)),
        out_shape=[jax.ShapeDtypeStruct((2, planes, strip + EDGE, Y), jnp.float32)] * group,
        in_specs=[smem, smem] + whole(1),
        out_specs=whole(group),
        compiler_params=params,
        scratch_shapes=[pltpu.VMEM((Y // LANES, 2, planes, X, LANES), jnp.float32)],
    )(corner_all, spot, got)
    moved = [parts[0]]
    for step in range(1, group):
        pairs = [
            (s * CORES + c, (s + step // CORES) % sides * CORES + (c + step) % CORES)
            for s in range(sides)
            for c in range(CORES)
        ]
        moved.append(lax.ppermute(parts[step], ("side", "core"), pairs))

    face = jax.ShapeDtypeStruct((strip, Y), jnp.float32)
    cells, low, high = pl.pallas_call(
        functools.partial(normal_kernel, (planes, strip, group)),
        out_shape=[jax.ShapeDtypeStruct((planes * CORES, strip + EDGE, Y), jnp.float32), face, face],
        in_specs=[smem] + whole(group),
        out_specs=whole(3),
        compiler_params=params,
    )(spot, *moved)
    under = lax.ppermute(high, "tile", [(t, t + 1) for t in range(tiles - 1)])
    over = lax.ppermute(low, "tile", [(t + 1, t) for t in range(tiles - 1)])
    inner_shape = jax.ShapeDtypeStruct((planes * CORES, strip, Y), jnp.float32)
    inner = pl.pallas_call(
        functools.partial(lateral_kernel, (planes * CORES, strip)),
        out_shape=inner_shape,
        in_specs=whole(1),
        out_specs=whole(1)[0],
        compiler_params=params,
        cost_estimate=pl.CostEstimate(flops=COVER, bytes_accessed=1 << 20, transcendentals=0),
    )(cells)
    return pl.pallas_call(
        faces_kernel,
        out_shape=inner_shape,
        in_specs=whole(3),
        out_specs=whole(1)[0],
        compiler_params=params,
    )(inner, under, over)


def solution(mesh):
    shot_count, tile_count = mesh.devices.shape
    fine = Mesh(mesh.devices.reshape(shot_count // CORES, CORES, tile_count), ("side", "core", "tile"))
    split = ("side", "core", "tile")
    return jax.shard_map(
        per_device,
        mesh=fine,
        in_specs=(P(split, None, None, None, None), P(split, None, None, None, None), P(split, None)),
        out_specs=P("tile", ("side", "core"), None),
        check_vma=False,
    )
```

time: 72 us -> 67.4 us (0.936); the launches traced: 71.7 us -> 66.1 us
  other arithmetic: 3.12 us -> 0.08 us
  Pallas kernels: 8.16 us -> 5.94 us
    pallas_call x1, Pallas kernels: 4.12 us -> 2.56 us  [per_device(): pl.pallas_call(functools.partial(place_kernel, (shots, times, planes, row...]
    convert_element_type x2 -> x1, other arithmetic: 1.39 us -> 0.01 us  [per_device(): corner_all = got[:, -2 * EDGE, :2 * shots].astype(jnp.int32)]
    reshape x3 -> x0, local copies, waits for them, and re-layouts: 1.2 us -> none  [the longest x2 1.11 us: per_device(): field.reshape(shots, times, spread, planes, rows, cols)]
    ppermute x4 -> x5, waiting for transfers between devices: 18.4 us -> 17.2 us  [the longest x3 13 us: per_device(): moved.append(lax.ppermute(parts[step], ('side', 'core'), pairs))]
    concatenate x1 -> x0, other arithmetic: 1.08 us -> none  [per_device(): packed = jnp.concatenate(fields + [tag], axis=1)]
    unnamed x12 -> x6, local copies, waits for them, and re-layouts: 1.84 us -> 2.76 us
    pallas_call x2 -> x4, Pallas kernels: 4.04 us -> 3.39 us  [the longest x1 1.79 us: per_device(): pl.pallas_call(pack_kernel, out_shape=jax.ShapeDtypeStruct((spread, block...]
    ppermute x4 -> x5, starting transfers between devices: 8.13 us -> 8.7 us  [the longest x1 4.58 us: per_device(): under = lax.ppermute(high, 'tile', [(t, t + 1) for t in range(tiles - 1)])]
  transfers between devices with their start and end apart: 5 -> 6, of which waited for: 3 -> 4; matrix products, arithmetic and copies ran while one was open for 1% -> 0% of each run, Pallas kernels for 0% -> 0%
where the time goes in v3:
time: 67.4 us; the launch traced here: 66.1 us
  waiting for transfers between devices  41.9 us (62%)
  starting transfers between devices  15.3 us (23%)
  Pallas kernels  5.94 us (9%)
  local copies, waits for them, and re-layouts  2.76 us (4%)
    all_to_all x1, waiting for transfers between devices, per_device(): lax.all_to_all(packed, ('tile', 'core'), split_axis=0, concat_axis=0, til...  24.7 us
    ppermute x3, waiting for transfers between devices, per_device(): moved.append(lax.ppermute(parts[step], ('side', 'core'), pairs))  13 us
    all_to_all x1, starting transfers between devices, per_device(): lax.all_to_all(packed, ('tile', 'core'), split_axis=0, concat_axis=0, til...  6.65 us
    ppermute x1, starting transfers between devices, per_device(): under = lax.ppermute(high, 'tile', [(t, t + 1) for t in range(tiles - 1)])  4.58 us
    ppermute x1, waiting for transfers between devices, per_device(): over = lax.ppermute(low, 'tile', [(t + 1, t) for t in range(tiles - 1)])  4.21 us
    unnamed x6, local copies, waits for them, and re-layouts  2.76 us
    pallas_call x1, Pallas kernels, per_device(): pl.pallas_call(functools.partial(place_kernel, (shots, times, planes, row...  2.56 us
    ppermute x3, starting transfers between devices, per_device(): moved.append(lax.ppermute(parts[step], ('side', 'core'), pairs))  2.2 us
  transfers between devices with their start and end apart: 6, of which 4 were waited for; matrix products, arithmetic and copies ran while one was open for 0% of the time, Pallas kernels for 0%

profile of v3, /device:TPU:3, one launch (start us, length us, event | category | flops | bytes accessed | tf_op | source)
XLA Modules:
  0.0 66.1 jit_solution(15155804384078638685)
XLA Ops:
  0.0 0.0 copy-start
  0.0 1.0 %copy-done = bf16[2,1,32,32,128]{4,3,2,1,0:T(8,128)(2,1)S(1)} copy-done((bf16[2,1,32,32,128]{4,3,2,1,0:T(8,128)(2,1)S(1)}, bf16[2,1,32,32,128]{4,3,2,1,0:T(8,128)(2,1)}, u32[]{:S(2)}) %copy-start) | copy-done | bytes 524312
  1.0 0.0 copy-start.1
  1.0 1.0 %copy-done.1 = bf16[2,1,32,32,128]{4,3,2,1,0:T(8,128)(2,1)S(1)} copy-done((bf16[2,1,32,32,128]{4,3,2,1,0:T(8,128)(2,1)S(1)}, bf16[2,1,32,32,128]{4,3,2,1,0:T(8,128)(2,1)}, u32[]{:S(2)}) %copy-start.1) | copy-done | bytes 524312
  2.1 0.0 copy-start.2
  2.1 0.7 %copy-done.2 = s32[2,2]{1,0:T(2,128)S(1)} copy-done((s32[2,2]{1,0:T(2,128)S(1)}, s32[2,2]{1,0:T(2,128)}, u32[]{:S(2)}) %copy-start.2) | copy-done | bytes 40
  2.8 1.8 %shard_map.37 = bf16[16,272,128]{2,1,0:T(8,128)(2,1)} custom-call(s32[2,2]{1,0:T(2,128)S(1)} %copy-done.2, bf16[2,1,16,2,32,128]{5,4,3,2,1,0:T(8,128)(2,1)S(1)} %bitcast.5, bf16[2,1,16,2,32,128]{5,4,3,2,1,0:T(8,128)(2,1)S(1)} %bitcast.6), custom_call_target="tpu_custom_call" | custom-call | tf_op jit(solution)/shard_map/pallas_call | solution.py:175
  4.6 6.6 %all-to-all-start = ((bf16[16,272,128]{2,1,0:T(8,128)(2,1)}), bf16[16,272,128]{2,1,0:T(8,128)(2,1)S(1)}, u32[]{:S(2)}, u32[]{:S(2)}) async-start(bf16[16,272,128]{2,1,0:T(8,128)(2,1)} %shard_map.37), calls=%async_computation | async-start | bytes 2228224 | tf_op jit(solution)/shard_map/all_to_all | solution.py:183
  11.2 0.1 pad_add_fusion.spot_ref
  11.3 24.7 %all-to-all-done.got_ref = bf16[16,272,128]{2,1,0:T(8,128)(2,1)S(1)} async-done(((bf16[16,272,128]{2,1,0:T(8,128)(2,1)}), bf16[16,272,128]{2,1,0:T(8,128)(2,1)S(1)}, u32[]{:S(2)}, u32[]{:S(2)}) %all-to-all-start) | async-done | bytes 1114144 | tf_op jit(solution)/shard_map/all_to_all | solution.py:183
  36.0 2.6 %shard_map.38 = (f32[2,2,72,256]{3,2,1,0:T(8,128)S(1)}, f32[2,2,72,256]{3,2,1,0:T(8,128)S(1)}, f32[2,2,72,256]{3,2,1,0:T(8,128)S(1)}, f32[2,2,72,256]{3,2,1,0:T(8,128)S(1)}) custom-call(s32[16,4]{1,0:T(8,128)S(1)} %bitcast.7, s32[2]{0:T(128)S(1)} %pad_add_fusion.spot_ref, bf16[16,272,128]{2,1,0:T(8,128)(2,1)S(1)} %all-to-all-done.got_ref), custom_call_target="tpu_custom_call" | custom-call | tf_op jit(solution)/shard_map/pallas_call | solution.py:187
  38.5 0.1 collective-permute-start
  38.6 1.3 %collective-permute-start.1 = (f32[2,2,72,256]{3,2,1,0:T(8,128)S(1)}, f32[2,2,72,256]{3,2,1,0:T(8,128)S(1)}, u32[]{:S(2)}, u32[]{:S(2)}) collective-permute-start(f32[2,2,72,256]{3,2,1,0:T(8,128)S(1)} %get-tuple-element.14), channel_id=1, source_target_pairs={{0,16},{8,24},{16,0},{24,8},{1,17},{9,25},{17,1},{25,9},{2,18},{10... | collective-permute-start | bytes 884744 | tf_op jit(solution)/shard_map/ppermute | solution.py:202
  39.9 0.8 %collective-permute-start.2 = (f32[2,2,72,256]{3,2,1,0:T(8,128)S(1)}, f32[2,2,72,256]{3,2,1,0:T(8,128)S(1)}, u32[]{:S(2)}, u32[]{:S(2)}) collective-permute-start(f32[2,2,72,256]{3,2,1,0:T(8,128)S(1)} %get-tuple-element.15), channel_id=1, source_target_pairs={{0,24},{8,16},{16,8},{24,0},{1,25},{9,17},{17,9},{25,1},{2,26},{10... | collective-permute-start | bytes 884744 | tf_op jit(solution)/shard_map/ppermute | solution.py:202
  40.8 0.0 collective-permute-done.refs_1_
  40.8 6.1 %collective-permute-done.1.refs_2_ = f32[2,2,72,256]{3,2,1,0:T(8,128)S(1)} collective-permute-done((f32[2,2,72,256]{3,2,1,0:T(8,128)S(1)}, f32[2,2,72,256]{3,2,1,0:T(8,128)S(1)}, u32[]{:S(2)}, u32[]{:S(2)}) %collective-permute-start.1) | collective-permute-done | bytes 294944 | tf_op jit(solution)/shard_map/ppermute | solution.py:202
  46.8 6.9 %collective-permute-done.2.refs_3_ = f32[2,2,72,256]{3,2,1,0:T(8,128)S(1)} collective-permute-done((f32[2,2,72,256]{3,2,1,0:T(8,128)S(1)}, f32[2,2,72,256]{3,2,1,0:T(8,128)S(1)}, u32[]{:S(2)}, u32[]{:S(2)}) %collective-permute-start.2) | collective-permute-done | bytes 294944 | tf_op jit(solution)/shard_map/ppermute | solution.py:202
  53.7 0.7 shard_map.39
  54.4 4.6 %collective-permute-start.3 = (f32[64,256]{1,0:T(8,128)S(1)}, f32[64,256]{1,0:T(8,128)S(1)}, u32[]{:S(2)}, u32[]{:S(2)}) collective-permute-start(f32[64,256]{1,0:T(8,128)S(1)} %get-tuple-element.17), channel_id=1, source_target_pairs={{0,1},{1,2},{2,3},{3,4},{4,5},{5,6},{6,7},{8,9},{9,10},{10,11},{11... | collective-permute-start | bytes 196616 | tf_op jit(solution)/shard_map/ppermute | solution.py:212
  59.0 1.9 %collective-permute-start.4 = (f32[64,256]{1,0:T(8,128)S(1)}, f32[64,256]{1,0:T(8,128)S(1)}, u32[]{:S(2)}, u32[]{:S(2)}) collective-permute-start(f32[64,256]{1,0:T(8,128)S(1)} %get-tuple-element.18), channel_id=1, source_target_pairs={{1,0},{2,1},{3,2},{4,3},{5,4},{6,5},{7,6},{9,8},{10,9},{11,10},{12... | collective-permute-start | bytes 196616 | tf_op jit(solution)/shard_map/ppermute | solution.py:213
  60.9 0.2 shard_map.40.inner
  61.1 0.0 collective-permute-done.3.under
  61.2 4.2 %collective-permute-done.4.over = f32[64,256]{1,0:T(8,128)S(1)} collective-permute-done((f32[64,256]{1,0:T(8,128)S(1)}, f32[64,256]{1,0:T(8,128)S(1)}, u32[]{:S(2)}, u32[]{:S(2)}) %collective-permute-start.4) | collective-permute-done | bytes 65568 | tf_op jit(solution)/shard_map/ppermute | solution.py:213
  65.4 0.7 %shard_map.41 = f32[4,64,256]{2,1,0:T(8,128)} custom-call(f32[4,64,256]{2,1,0:T(8,128)S(1)} %shard_map.40.inner, f32[64,256]{1,0:T(8,128)S(1)} %collective-permute-done.3.under, f32[64,256]{1,0:T(8,128)S(1)} %collective-permute-done.4.over), custom_call_target="tpu_custom_call" | custom-call | tf_op jit(solution)/shard_map/pallas_call | solution.py:223
  (1 shorter events, 0.0 us)
Async XLA Ops:
  0.0 1.0 %copy-start = (bf16[2,1,32,32,128]{4,3,2,1,0:T(8,128)(2,1)S(1)}, bf16[2,1,32,32,128]{4,3,2,1,0:T(8,128)(2,1)}, u32[]{:S(2)}) copy-start(bf16[2,1,32,32,128]{4,3,2,1,0:T(8,128)(2,1)} %param.3) | copy-start | bytes 1572868
  1.0 1.0 %copy-start.1 = (bf16[2,1,32,32,128]{4,3,2,1,0:T(8,128)(2,1)S(1)}, bf16[2,1,32,32,128]{4,3,2,1,0:T(8,128)(2,1)}, u32[]{:S(2)}) copy-start(bf16[2,1,32,32,128]{4,3,2,1,0:T(8,128)(2,1)} %param.4) | copy-start | bytes 1572868
  2.1 0.7 %copy-start.2 = (s32[2,2]{1,0:T(2,128)S(1)}, s32[2,2]{1,0:T(2,128)}, u32[]{:S(2)}) copy-start(s32[2,2]{1,0:T(2,128)} %corner_ref.1) | copy-start | bytes 52
  4.6 31.4 %all-to-all-start = ((bf16[16,272,128]{2,1,0:T(8,128)(2,1)}), bf16[16,272,128]{2,1,0:T(8,128)(2,1)S(1)}, u32[]{:S(2)}, u32[]{:S(2)}) async-start(bf16[16,272,128]{2,1,0:T(8,128)(2,1)} %shard_map.37), calls=%async_computation | async-start | bytes 2228224 | tf_op jit(solution)/shard_map/all_to_all | solution.py:183
  38.5 2.2 %collective-permute-start = (f32[2,2,72,256]{3,2,1,0:T(8,128)S(1)}, f32[2,2,72,256]{3,2,1,0:T(8,128)S(1)}, u32[]{:S(2)}, u32[]{:S(2)}) collective-permute-start(f32[2,2,72,256]{3,2,1,0:T(8,128)S(1)} %get-tuple-element.13), channel_id=1, source_target_pairs={{0,8},{8,0},{16,24},{24,16},{1,9},{9,1},{17,25},{25,17},{2,10},{10... | collective-permute-start | bytes 884744 | tf_op jit(solution)/shard_map/ppermute | solution.py:202
  38.6 8.2 %collective-permute-start.1 = (f32[2,2,72,256]{3,2,1,0:T(8,128)S(1)}, f32[2,2,72,256]{3,2,1,0:T(8,128)S(1)}, u32[]{:S(2)}, u32[]{:S(2)}) collective-permute-start(f32[2,2,72,256]{3,2,1,0:T(8,128)S(1)} %get-tuple-element.14), channel_id=1, source_target_pairs={{0,16},{8,24},{16,0},{24,8},{1,17},{9,25},{17,1},{25,9},{2,18},{10... | collective-permute-start | bytes 884744 | tf_op jit(solution)/shard_map/ppermute | solution.py:202
  39.9 13.8 %collective-permute-start.2 = (f32[2,2,72,256]{3,2,1,0:T(8,128)S(1)}, f32[2,2,72,256]{3,2,1,0:T(8,128)S(1)}, u32[]{:S(2)}, u32[]{:S(2)}) collective-permute-start(f32[2,2,72,256]{3,2,1,0:T(8,128)S(1)} %get-tuple-element.15), channel_id=1, source_target_pairs={{0,24},{8,16},{16,8},{24,0},{1,25},{9,17},{17,9},{25,1},{2,26},{10... | collective-permute-start | bytes 884744 | tf_op jit(solution)/shard_map/ppermute | solution.py:202
  54.4 6.7 %collective-permute-start.3 = (f32[64,256]{1,0:T(8,128)S(1)}, f32[64,256]{1,0:T(8,128)S(1)}, u32[]{:S(2)}, u32[]{:S(2)}) collective-permute-start(f32[64,256]{1,0:T(8,128)S(1)} %get-tuple-element.17), channel_id=1, source_target_pairs={{0,1},{1,2},{2,3},{3,4},{4,5},{5,6},{6,7},{8,9},{9,10},{10,11},{11... | collective-permute-start | bytes 196616 | tf_op jit(solution)/shard_map/ppermute | solution.py:212
  59.0 6.4 %collective-permute-start.4 = (f32[64,256]{1,0:T(8,128)S(1)}, f32[64,256]{1,0:T(8,128)S(1)}, u32[]{:S(2)}, u32[]{:S(2)}) collective-permute-start(f32[64,256]{1,0:T(8,128)S(1)} %get-tuple-element.18), channel_id=1, source_target_pairs={{1,0},{2,1},{3,2},{4,3},{5,4},{6,5},{7,6},{9,8},{10,9},{11,10},{12... | collective-permute-start | bytes 196616 | tf_op jit(solution)/shard_map/ppermute | solution.py:213

commit v4 on v3

--- a/solution.py
+++ b/solution.py
@@ -13,7 +13,6 @@
 CORES = 2
 EDGE = 8
 GRANT = 12 << 20
-COVER = 10 ** 7
 
 damping = 1.0
 
@@ -25,6 +24,7 @@
 def place_kernel(dims, corner_ref, spot_ref, got_ref, *refs):
     shots, times, planes, rows, sides, half = dims
     outs, total = refs[:-1], refs[-1]
+    outs = list(zip(outs[::2], outs[1::2]))
     senders = got_ref.shape[0]
     field = shots * times * planes * rows
     total[...] = jnp.zeros_like(total)
@@ -63,22 +63,24 @@
     core = spot_ref[1]
     strip = half // CORES
     slot = lax.broadcasted_iota(jnp.int32, (EDGE, LANES), 0)
-    for step, out in enumerate(outs):
+    for step, (outer, inner) in enumerate(outs):
         target = lax.rem(side + step // CORES, sides) * CORES + lax.rem(core + step % CORES, CORES)
         start = pl.multiple_of(target * strip, strip)
         before = pl.multiple_of(lax.max(start - EDGE, 0), EDGE)
         after = pl.multiple_of(lax.min(start + strip, X - EDGE), EDGE)
+        moves = [(outer, 0, core * (planes - 1))]
+        moves += [(inner, at, at + 1 - core) for at in range(planes - 1)]
         for kind in range(2):
-            for plane in range(planes):
+            for out, at, plane in moves:
                 for tile in range(Y // LANES):
                     lanes = slice(tile * LANES, (tile + 1) * LANES)
-                    out[kind, plane, :strip, lanes] = total[tile, kind, plane, pl.ds(start, strip), :]
+                    out[kind, at, :strip, lanes] = total[tile, kind, plane, pl.ds(start, strip), :]
                     above = total[tile, kind, plane, pl.ds(before, EDGE), :]
                     below = total[tile, kind, plane, pl.ds(after, EDGE), :]
                     above = jnp.where(target > 0, above, 0.0)
                     below = jnp.where(target < sides * CORES - 1, below, 0.0)
                     pair = jnp.where(slot == EDGE - 1, above, jnp.where(slot == 0, below, 0.0))
-                    out[kind, plane, strip:, lanes] = pair
+                    out[kind, at, strip:, lanes] = pair
 
 
 def pack_kernel(corner_ref, source, receiver, out, sems):
@@ -109,26 +111,37 @@
         copy.wait()
 
 
-def normal_kernel(dims, spot_ref, *refs):
-    planes, strip, parts = dims
-    ins, (cells, low, high) = refs[:parts], refs[parts:]
+def normal_of(ins, turn):
+    image = ins[turn][0]
+    light = ins[turn][1]
+    for part in ins[turn + CORES::CORES]:
+        image = image + part[0]
+        light = light + part[1]
+    return image / (damping + light)
+
+
+def outer_kernel(dims, spot_ref, *refs):
+    strip, parts = dims
+    ins, (ends, low, high) = refs[:parts], refs[parts:]
     core = spot_ref[1]
     for turn in range(CORES):
-        base = lax.rem(core + turn, CORES) * planes
-        image = ins[turn][0]
-        light = ins[turn][1]
-        for part in ins[turn + CORES::CORES]:
-            image = image + part[0]
-            light = light + part[1]
-        normal = image / (damping + light)
-        for plane in range(planes):
+        ends[lax.rem(core + turn, CORES)] = normal_of(ins, turn)[0]
+    low[...] = ends[0, :strip, :]
+    high[...] = ends[1, :strip, :]
+
+
+def laplace_kernel(dims, spot_ref, ends, under, over, *refs):
+    planes, strip, parts = dims
+    ins, (out, cells) = refs[:parts], refs[parts:]
+    depth = planes * CORES
+    core = spot_ref[1]
+    cells[0] = ends[0]
+    cells[depth - 1] = ends[1]
+    for turn in range(CORES):
+        normal = normal_of(ins, turn)
+        base = lax.rem(core + turn, CORES) * (planes - 1) + 1
+        for plane in range(planes - 1):
             cells[base + plane] = normal[plane]
-    low[...] = cells[0, :strip, :]
-    high[...] = cells[planes * CORES - 1, :strip, :]
-
-
-def lateral_kernel(dims, cells, out):
-    depth, strip = dims
     row = lax.broadcasted_iota(jnp.int32, (strip, Y), 0)
     col = lax.broadcasted_iota(jnp.int32, (strip, Y), 1)
     for plane in range(depth):
@@ -137,23 +150,9 @@
         below = jnp.where(row == strip - 1, cells[plane, strip:strip + 1, :], pltpu.roll(body, strip - 1, 0))
         left = jnp.where(col == 0, 0.0, pltpu.roll(body, 1, 1))
         right = jnp.where(col == Y - 1, 0.0, pltpu.roll(body, Y - 1, 1))
-        value = above + below + left + right - 6.0 * body
-        if plane > 0:
-            value = value + cells[plane - 1, :strip, :]
-        if plane < depth - 1:
-            value = value + cells[plane + 1, :strip, :]
-        out[plane] = value
-
-
-def faces_kernel(inner, under, over, out):
-    depth = inner.shape[0]
-    for plane in range(depth):
-        value = inner[plane]
-        if plane == 0:
-            value = value + under[...]
-        if plane == depth - 1:
-            value = value + over[...]
-        out[plane] = value
+        down = under[...] if plane == 0 else cells[plane - 1, :strip, :]
+        up = over[...] if plane == depth - 1 else cells[plane + 1, :strip, :]
+        out[plane] = above + below + left + right + down + up - 6.0 * body
 
 
 def per_device(source, receiver, corners):
@@ -178,55 +177,50 @@
         in_specs=[smem] + [pl.BlockSpec(memory_space=pltpu.HBM)] * 2,
         out_specs=pl.BlockSpec(memory_space=pltpu.VMEM),
         scratch_shapes=[pltpu.SemaphoreType.DMA((blocks,))],
-        compiler_params=params,
     )(corners, *raw)
     got = lax.all_to_all(packed, ("tile", "core"), split_axis=0, concat_axis=0, tiled=True)
     corner_all = got[:, -2 * EDGE, : 2 * shots].astype(jnp.int32)
 
     group = sides * CORES
+    shapes = [
+        jax.ShapeDtypeStruct((2, count, strip + EDGE, Y), jnp.float32) for count in (1, planes - 1)
+    ]
     parts = pl.pallas_call(
         functools.partial(place_kernel, (shots, times, planes, rows, sides, half)),
-        out_shape=[jax.ShapeDtypeStruct((2, planes, strip + EDGE, Y), jnp.float32)] * group,
+        out_shape=shapes * group,
         in_specs=[smem, smem] + whole(1),
-        out_specs=whole(group),
+        out_specs=whole(2 * group),
         compiler_params=params,
         scratch_shapes=[pltpu.VMEM((Y // LANES, 2, planes, X, LANES), jnp.float32)],
     )(corner_all, spot, got)
-    moved = [parts[0]]
-    for step in range(1, group):
-        pairs = [
-            (s * CORES + c, (s + step // CORES) % sides * CORES + (c + step) % CORES)
-            for s in range(sides)
-            for c in range(CORES)
-        ]
-        moved.append(lax.ppermute(parts[step], ("side", "core"), pairs))
+    outers, inners = list(parts[::2]), list(parts[1::2])
+    for held in (outers, inners):
+        for step in range(1, group):
+            pairs = [
+                (s * CORES + c, (s + step // CORES) % sides * CORES + (c + step) % CORES)
+                for s in range(sides)
+                for c in range(CORES)
+            ]
+            held[step] = lax.ppermute(held[step], ("side", "core"), pairs)
 
     face = jax.ShapeDtypeStruct((strip, Y), jnp.float32)
-    cells, low, high = pl.pallas_call(
-        functools.partial(normal_kernel, (planes, strip, group)),
-        out_shape=[jax.ShapeDtypeStruct((planes * CORES, strip + EDGE, Y), jnp.float32), face, face],
+    ends, low, high = pl.pallas_call(
+        functools.partial(outer_kernel, (strip, group)),
+        out_shape=[jax.ShapeDtypeStruct((2, strip + EDGE, Y), jnp.float32), face, face],
         in_specs=[smem] + whole(group),
         out_specs=whole(3),
         compiler_params=params,
-    )(spot, *moved)
+    )(spot, *outers)
     under = lax.ppermute(high, "tile", [(t, t + 1) for t in range(tiles - 1)])
     over = lax.ppermute(low, "tile", [(t + 1, t) for t in range(tiles - 1)])
-    inner_shape = jax.ShapeDtypeStruct((planes * CORES, strip, Y), jnp.float32)
-    inner = pl.pallas_call(
-        functools.partial(lateral_kernel, (planes * CORES, strip)),
-        out_shape=inner_shape,
-        in_specs=whole(1),
+    return pl.pallas_call(
+        functools.partial(laplace_kernel, (planes, strip, group)),
+        out_shape=jax.ShapeDtypeStruct((planes * CORES, strip, Y), jnp.float32),
+        in_specs=[smem] + whole(3 + group),
         out_specs=whole(1)[0],
+        scratch_shapes=[pltpu.VMEM((planes * CORES, strip + EDGE, Y), jnp.float32)],
         compiler_params=params,
-        cost_estimate=pl.CostEstimate(flops=COVER, bytes_accessed=1 << 20, transcendentals=0),
-    )(cells)
-    return pl.pallas_call(
-        faces_kernel,
-        out_shape=inner_shape,
-        in_specs=whole(3),
-        out_specs=whole(1)[0],
-        compiler_params=params,
-    )(inner, under, over)
+    )(spot, ends, under, over, *inners)
 
 
 def solution(mesh):

time: 67.4 us -> 60.7 us (0.901)
  waiting for transfers between devices: 41.9 us -> 34.6 us
  local copies, waits for them, and re-layouts: 2.76 us -> 0 us
  starting transfers between devices: 15.3 us -> 17.5 us
  Pallas kernels: 5.94 us -> 7.71 us
    ppermute x3 -> x6, waiting for transfers between devices: 13 us -> 5.42 us  [per_device(): held[step] = lax.ppermute(held[step], ('side', 'core'), pairs)]
    unnamed x6 -> x0, local copies, waits for them, and re-layouts: 2.76 us -> none
    ppermute x3 -> x6, starting transfers between devices: 2.2 us -> 4.34 us  [per_device(): held[step] = lax.ppermute(held[step], ('side', 'core'), pairs)]
    pallas_call x1, Pallas kernels: 1.79 us -> 3.03 us  [per_device(): pl.pallas_call(pack_kernel, out_shape=jax.ShapeDtypeStruct((spread, block...]
    pallas_call x3 -> x2, Pallas kernels: 1.59 us -> 2.12 us  [the longest x1 1.53 us: per_device(): pl.pallas_call(functools.partial(laplace_kernel, (planes, strip, group)),...]
  transfers between devices with their start and end apart: 6 -> 9, of which waited for: 4 -> 4; matrix products, arithmetic and copies ran while one was open for 0% -> 0% of each run, Pallas kernels for 0% -> 1%
where the time goes in v4:
time: 60.7 us; the launch traced here: 59.9 us
  waiting for transfers between devices  34.6 us (57%)
  starting transfers between devices  17.5 us (29%)
  Pallas kernels  7.71 us (13%)
    all_to_all x1, waiting for transfers between devices, per_device(): lax.all_to_all(packed, ('tile', 'core'), split_axis=0, concat_axis=0, til...  24.7 us
    all_to_all x1, starting transfers between devices, per_device(): lax.all_to_all(packed, ('tile', 'core'), split_axis=0, concat_axis=0, til...  6.65 us
    ppermute x6, waiting for transfers between devices, per_device(): held[step] = lax.ppermute(held[step], ('side', 'core'), pairs)  5.42 us
    ppermute x1, starting transfers between devices, per_device(): under = lax.ppermute(high, 'tile', [(t, t + 1) for t in range(tiles - 1)])  4.58 us
    ppermute x1, waiting for transfers between devices, per_device(): over = lax.ppermute(low, 'tile', [(t + 1, t) for t in range(tiles - 1)])  4.46 us
    ppermute x6, starting transfers between devices, per_device(): held[step] = lax.ppermute(held[step], ('side', 'core'), pairs)  4.34 us
    pallas_call x1, Pallas kernels, per_device(): pl.pallas_call(pack_kernel, out_shape=jax.ShapeDtypeStruct((spread, block...  3.03 us
    pallas_call x1, Pallas kernels, per_device(): pl.pallas_call(functools.partial(place_kernel, (shots, times, planes, row...  2.56 us
  transfers between devices with their start and end apart: 9, of which 4 were waited for; matrix products, arithmetic and copies ran while one was open for 0% of the time, Pallas kernels for 1%

profile of v4, /device:TPU:3, one launch (start us, length us, event | category | flops | bytes accessed | tf_op | source)
XLA Modules:
  0.0 59.9 jit_solution(1188386060439312830)
XLA Ops:
  0.0 3.0 %shard_map.37 = bf16[16,272,128]{2,1,0:T(8,128)(2,1)} custom-call(s32[2,2]{1,0:T(2,128)} %corner_ref.1, bf16[2,1,16,2,32,128]{5,4,3,2,1,0:T(8,128)(2,1)} %bitcast.6, bf16[2,1,16,2,32,128]{5,4,3,2,1,0:T(8,128)(2,1)} %bitcast.7), custom_call_target="tpu_custom_call" | custom-call | tf_op jit(solution)/shard_map/pallas_call | solution.py:174
  3.0 6.6 %all-to-all-start = ((bf16[16,272,128]{2,1,0:T(8,128)(2,1)}), bf16[16,272,128]{2,1,0:T(8,128)(2,1)S(1)}, u32[]{:S(2)}, u32[]{:S(2)}) async-start(bf16[16,272,128]{2,1,0:T(8,128)(2,1)} %shard_map.37), calls=%async_computation | async-start | bytes 2228224 | tf_op jit(solution)/shard_map/all_to_all | solution.py:181
  9.7 0.1 pad_add_fusion.spot_ref
  9.8 24.7 %all-to-all-done.got_ref = bf16[16,272,128]{2,1,0:T(8,128)(2,1)S(1)} async-done(((bf16[16,272,128]{2,1,0:T(8,128)(2,1)}), bf16[16,272,128]{2,1,0:T(8,128)(2,1)S(1)}, u32[]{:S(2)}, u32[]{:S(2)}) %all-to-all-start) | async-done | bytes 1114144 | tf_op jit(solution)/shard_map/all_to_all | solution.py:181
  34.5 2.6 %shard_map.38 = (f32[2,1,72,256]{3,2,1,0:T(8,128)S(1)}, f32[2,1,72,256]{3,2,1,0:T(8,128)S(1)}, f32[2,1,72,256]{3,2,1,0:T(8,128)S(1)}, f32[2,1,72,256]{3,2,1,0:T(...) custom-call(s32[16,4]{1,0:T(8,128)S(1)} %bitcast.5, ...), custom_call_target="tpu_custom_call" | custom-call | tf_op jit(solution)/shard_map/pallas_call | solution.py:188
  37.0 0.1 collective-permute-start
  37.1 1.3 %collective-permute-start.1 = (f32[2,1,72,256]{3,2,1,0:T(8,128)S(1)}, f32[2,1,72,256]{3,2,1,0:T(8,128)S(1)}, u32[]{:S(2)}, u32[]{:S(2)}) collective-permute-start(f32[2,1,72,256]{3,2,1,0:T(8,128)S(1)} %get-tuple-element.18), channel_id=1, source_target_pairs={{0,16},{8,24},{16,0},{24,8},{1,17},{9,25},{17,1},{25,9},{2,18},{10... | collective-permute-start | bytes 442376 | tf_op jit(solution)/shard_map/ppermute | solution.py:204
  38.4 0.8 %collective-permute-start.2 = (f32[2,1,72,256]{3,2,1,0:T(8,128)S(1)}, f32[2,1,72,256]{3,2,1,0:T(8,128)S(1)}, u32[]{:S(2)}, u32[]{:S(2)}) collective-permute-start(f32[2,1,72,256]{3,2,1,0:T(8,128)S(1)} %get-tuple-element.19), channel_id=1, source_target_pairs={{0,24},{8,16},{16,8},{24,0},{1,25},{9,17},{17,9},{25,1},{2,26},{10... | collective-permute-start | bytes 442376 | tf_op jit(solution)/shard_map/ppermute | solution.py:204
  39.2 0.0 collective-permute-start.5
  39.2 1.2 %collective-permute-start.6 = (f32[2,1,72,256]{3,2,1,0:T(8,128)S(1)}, f32[2,1,72,256]{3,2,1,0:T(8,128)S(1)}, u32[]{:S(2)}, u32[]{:S(2)}) collective-permute-start(f32[2,1,72,256]{3,2,1,0:T(8,128)S(1)} %get-tuple-element.25), channel_id=1, source_target_pairs={{0,16},{8,24},{16,0},{24,8},{1,17},{9,25},{17,1},{25,9},{2,18},{10... | collective-permute-start | bytes 442376 | tf_op jit(solution)/shard_map/ppermute | solution.py:204
  40.5 0.0 collective-permute-done.refs_1_
  40.5 0.9 %collective-permute-start.7 = (f32[2,1,72,256]{3,2,1,0:T(8,128)S(1)}, f32[2,1,72,256]{3,2,1,0:T(8,128)S(1)}, u32[]{:S(2)}, u32[]{:S(2)}) collective-permute-start(f32[2,1,72,256]{3,2,1,0:T(8,128)S(1)} %get-tuple-element.26), channel_id=1, source_target_pairs={{0,24},{8,16},{16,8},{24,0},{1,25},{9,17},{17,9},{25,1},{2,26},{10... | collective-permute-start | bytes 442376 | tf_op jit(solution)/shard_map/ppermute | solution.py:204
  41.4 0.8 %collective-permute-done.1.refs_2_ = f32[2,1,72,256]{3,2,1,0:T(8,128)S(1)} collective-permute-done((f32[2,1,72,256]{3,2,1,0:T(8,128)S(1)}, f32[2,1,72,256]{3,2,1,0:T(8,128)S(1)}, u32[]{:S(2)}, u32[]{:S(2)}) %collective-permute-start.1) | collective-permute-done | bytes 147488 | tf_op jit(solution)/shard_map/ppermute | solution.py:204
  42.1 4.6 %collective-permute-done.2.refs_3_ = f32[2,1,72,256]{3,2,1,0:T(8,128)S(1)} collective-permute-done((f32[2,1,72,256]{3,2,1,0:T(8,128)S(1)}, f32[2,1,72,256]{3,2,1,0:T(8,128)S(1)}, u32[]{:S(2)}, u32[]{:S(2)}) %collective-permute-start.2) | collective-permute-done | bytes 147488 | tf_op jit(solution)/shard_map/ppermute | solution.py:204
  46.8 0.6 shard_map.39
  47.4 4.6 %collective-permute-start.3 = (f32[64,256]{1,0:T(8,128)S(1)}, f32[64,256]{1,0:T(8,128)S(1)}, u32[]{:S(2)}, u32[]{:S(2)}) collective-permute-start(f32[64,256]{1,0:T(8,128)S(1)} %get-tuple-element.21), channel_id=1, source_target_pairs={{0,1},{1,2},{2,3},{3,4},{4,5},{5,6},{6,7},{8,9},{9,10},{10,11},{11... | collective-permute-start | bytes 196616 | tf_op jit(solution)/shard_map/ppermute | solution.py:214
  52.0 1.9 %collective-permute-start.4 = (f32[64,256]{1,0:T(8,128)S(1)}, f32[64,256]{1,0:T(8,128)S(1)}, u32[]{:S(2)}, u32[]{:S(2)}) collective-permute-start(f32[64,256]{1,0:T(8,128)S(1)} %get-tuple-element.22), channel_id=1, source_target_pairs={{1,0},{2,1},{3,2},{4,3},{5,4},{6,5},{7,6},{9,8},{10,9},{11,10},{12... | collective-permute-start | bytes 196616 | tf_op jit(solution)/shard_map/ppermute | solution.py:215
  53.9 0.0 collective-permute-done.5.refs_1_
  53.9 0.0 collective-permute-done.6.refs_2_
  53.9 0.0 collective-permute-done.7.refs_3_
  53.9 0.0 collective-permute-done.3.under
  54.0 4.5 %collective-permute-done.4.over = f32[64,256]{1,0:T(8,128)S(1)} collective-permute-done((f32[64,256]{1,0:T(8,128)S(1)}, f32[64,256]{1,0:T(8,128)S(1)}, u32[]{:S(2)}, u32[]{:S(2)}) %collective-permute-start.4) | collective-permute-done | bytes 65568 | tf_op jit(solution)/shard_map/ppermute | solution.py:215
  58.4 1.5 %shard_map.40 = f32[4,64,256]{2,1,0:T(8,128)} custom-call(s32[2]{0:T(128)S(1)} %pad_add_fusion.spot_ref, f32[2,72,256]{2,1,0:T(8,128)S(1)} %get-tuple-element.20.ends, f32[64,256]{1,0:T(8,128)S(1)} %collective-permute-done.3.under, f32[64,256]{1,0:T(8,128)S(1)} %collective-permute-done.4.over, f32[2,1,72,256]{3,2,1,0:T(8,128)S(1)} %get-tuple-element.23.refs_0_, ...), custom_call_target="tpu_custom_call" | custom-call | tf_op jit(solution)/shard_map/pallas_call | solution.py:216
  (1 shorter events, 0.0 us)
Async XLA Ops:
  3.0 31.4 %all-to-all-start = ((bf16[16,272,128]{2,1,0:T(8,128)(2,1)}), bf16[16,272,128]{2,1,0:T(8,128)(2,1)S(1)}, u32[]{:S(2)}, u32[]{:S(2)}) async-start(bf16[16,272,128]{2,1,0:T(8,128)(2,1)} %shard_map.37), calls=%async_computation | async-start | bytes 2228224 | tf_op jit(solution)/shard_map/all_to_all | solution.py:181
  37.0 3.5 %collective-permute-start = (f32[2,1,72,256]{3,2,1,0:T(8,128)S(1)}, f32[2,1,72,256]{3,2,1,0:T(8,128)S(1)}, u32[]{:S(2)}, u32[]{:S(2)}) collective-permute-start(f32[2,1,72,256]{3,2,1,0:T(8,128)S(1)} %get-tuple-element.17), channel_id=1, source_target_pairs={{0,8},{8,0},{16,24},{24,16},{1,9},{9,1},{17,25},{25,17},{2,10},{10... | collective-permute-start | bytes 442376 | tf_op jit(solution)/shard_map/ppermute | solution.py:204
  37.1 5.0 %collective-permute-start.1 = (f32[2,1,72,256]{3,2,1,0:T(8,128)S(1)}, f32[2,1,72,256]{3,2,1,0:T(8,128)S(1)}, u32[]{:S(2)}, u32[]{:S(2)}) collective-permute-start(f32[2,1,72,256]{3,2,1,0:T(8,128)S(1)} %get-tuple-element.18), channel_id=1, source_target_pairs={{0,16},{8,24},{16,0},{24,8},{1,17},{9,25},{17,1},{25,9},{2,18},{10... | collective-permute-start | bytes 442376 | tf_op jit(solution)/shard_map/ppermute | solution.py:204
  38.4 8.4 %collective-permute-start.2 = (f32[2,1,72,256]{3,2,1,0:T(8,128)S(1)}, f32[2,1,72,256]{3,2,1,0:T(8,128)S(1)}, u32[]{:S(2)}, u32[]{:S(2)}) collective-permute-start(f32[2,1,72,256]{3,2,1,0:T(8,128)S(1)} %get-tuple-element.19), channel_id=1, source_target_pairs={{0,24},{8,16},{16,8},{24,0},{1,25},{9,17},{17,9},{25,1},{2,26},{10... | collective-permute-start | bytes 442376 | tf_op jit(solution)/shard_map/ppermute | solution.py:204
  39.2 14.7 %collective-permute-start.5 = (f32[2,1,72,256]{3,2,1,0:T(8,128)S(1)}, f32[2,1,72,256]{3,2,1,0:T(8,128)S(1)}, u32[]{:S(2)}, u32[]{:S(2)}) collective-permute-start(f32[2,1,72,256]{3,2,1,0:T(8,128)S(1)} %get-tuple-element.24), channel_id=1, source_target_pairs={{0,8},{8,0},{16,24},{24,16},{1,9},{9,1},{17,25},{25,17},{2,10},{10... | collective-permute-start | bytes 442376 | tf_op jit(solution)/shard_map/ppermute | solution.py:204
  39.2 14.7 %collective-permute-start.6 = (f32[2,1,72,256]{3,2,1,0:T(8,128)S(1)}, f32[2,1,72,256]{3,2,1,0:T(8,128)S(1)}, u32[]{:S(2)}, u32[]{:S(2)}) collective-permute-start(f32[2,1,72,256]{3,2,1,0:T(8,128)S(1)} %get-tuple-element.25), channel_id=1, source_target_pairs={{0,16},{8,24},{16,0},{24,8},{1,17},{9,25},{17,1},{25,9},{2,18},{10... | collective-permute-start | bytes 442376 | tf_op jit(solution)/shard_map/ppermute | solution.py:204
  40.5 13.5 %collective-permute-start.7 = (f32[2,1,72,256]{3,2,1,0:T(8,128)S(1)}, f32[2,1,72,256]{3,2,1,0:T(8,128)S(1)}, u32[]{:S(2)}, u32[]{:S(2)}) collective-permute-start(f32[2,1,72,256]{3,2,1,0:T(8,128)S(1)} %get-tuple-element.26), channel_id=1, source_target_pairs={{0,24},{8,16},{16,8},{24,0},{1,25},{9,17},{17,9},{25,1},{2,26},{10... | collective-permute-start | bytes 442376 | tf_op jit(solution)/shard_map/ppermute | solution.py:204
  47.4 6.6 %collective-permute-start.3 = (f32[64,256]{1,0:T(8,128)S(1)}, f32[64,256]{1,0:T(8,128)S(1)}, u32[]{:S(2)}, u32[]{:S(2)}) collective-permute-start(f32[64,256]{1,0:T(8,128)S(1)} %get-tuple-element.21), channel_id=1, source_target_pairs={{0,1},{1,2},{2,3},{3,4},{4,5},{5,6},{6,7},{8,9},{9,10},{10,11},{11... | collective-permute-start | bytes 196616 | tf_op jit(solution)/shard_map/ppermute | solution.py:214
  52.0 6.4 %collective-permute-start.4 = (f32[64,256]{1,0:T(8,128)S(1)}, f32[64,256]{1,0:T(8,128)S(1)}, u32[]{:S(2)}, u32[]{:S(2)}) collective-permute-start(f32[64,256]{1,0:T(8,128)S(1)} %get-tuple-element.22), channel_id=1, source_target_pairs={{1,0},{2,1},{3,2},{4,3},{5,4},{6,5},{7,6},{9,8},{10,9},{11,10},{12... | collective-permute-start | bytes 196616 | tf_op jit(solution)/shard_map/ppermute | solution.py:215

commit v5 on v4

--- a/solution.py
+++ b/solution.py
@@ -84,20 +84,17 @@
 
 
 def pack_kernel(corner_ref, source, receiver, out, sems):
-    shots, times, spread, planes, rows, cols = source.shape
-    cell = planes * rows
+    shots, times, spread, cell, cols = source.shape
     copies = []
     for kind, field in enumerate((source, receiver)):
         for shot in range(shots):
             for time in range(times):
                 block = (kind * shots + shot) * times + time
-                for plane in range(planes):
-                    at = block * cell + plane * rows
-                    copy = pltpu.make_async_copy(
-                        field.at[shot, time, :, plane], out.at[:, at:at + rows, :], sems.at[block * planes + plane]
-                    )
-                    copy.start()
-                    copies.append(copy)
+                copy = pltpu.make_async_copy(
+                    field.at[shot, time], out.at[:, block * cell:(block + 1) * cell, :], sems.at[block]
+                )
+                copy.start()
+                copies.append(copy)
     lane = lax.broadcasted_iota(jnp.int32, (2 * EDGE, cols), 1)
     tag = jnp.zeros((2 * EDGE, cols), jnp.float32)
     for shot in range(shots):
@@ -122,19 +119,23 @@
 
 def outer_kernel(dims, spot_ref, *refs):
     strip, parts = dims
-    ins, (ends, low, high) = refs[:parts], refs[parts:]
+    ins, (ends, first, second) = refs[:parts], refs[parts:]
     core = spot_ref[1]
+    odd = spot_ref[2]
     for turn in range(CORES):
         ends[lax.rem(core + turn, CORES)] = normal_of(ins, turn)[0]
-    low[...] = ends[0, :strip, :]
-    high[...] = ends[1, :strip, :]
-
-
-def laplace_kernel(dims, spot_ref, ends, under, over, *refs):
+    first[...] = ends[1 - odd, :strip, :]
+    second[...] = ends[odd, :strip, :]
+
+
+def laplace_kernel(dims, spot_ref, ends, first, second, *refs):
     planes, strip, parts = dims
     ins, (out, cells) = refs[:parts], refs[parts:]
     depth = planes * CORES
     core = spot_ref[1]
+    even = spot_ref[2] == 0
+    under = jnp.where(even, second[...], first[...])
+    over = jnp.where(even, first[...], second[...])
     cells[0] = ends[0]
     cells[depth - 1] = ends[1]
     for turn in range(CORES):
@@ -150,8 +151,8 @@
         below = jnp.where(row == strip - 1, cells[plane, strip:strip + 1, :], pltpu.roll(body, strip - 1, 0))
         left = jnp.where(col == 0, 0.0, pltpu.roll(body, 1, 1))
         right = jnp.where(col == Y - 1, 0.0, pltpu.roll(body, Y - 1, 1))
-        down = under[...] if plane == 0 else cells[plane - 1, :strip, :]
-        up = over[...] if plane == depth - 1 else cells[plane + 1, :strip, :]
+        down = under if plane == 0 else cells[plane - 1, :strip, :]
+        up = over if plane == depth - 1 else cells[plane + 1, :strip, :]
         out[plane] = above + below + left + right + down + up - 6.0 * body
 
 
@@ -165,12 +166,12 @@
     strip = half // CORES
     side = lax.axis_index("side")
     core = lax.axis_index("core")
-    spot = jnp.stack([side, core]).astype(jnp.int32)
+    spot = jnp.stack([side, core, lax.axis_index("tile") % 2]).astype(jnp.int32)
     smem = pl.BlockSpec(memory_space=pltpu.SMEM)
     params = pltpu.CompilerParams(vmem_limit_bytes=GRANT)
 
     blocks = 2 * shots * times * planes
-    raw = [field.reshape(shots, times, spread, planes, rows, cols) for field in (source, receiver)]
+    raw = [field.reshape(shots, times, spread, planes * rows, cols) for field in (source, receiver)]
     packed = pl.pallas_call(
         pack_kernel,
         out_shape=jax.ShapeDtypeStruct((spread, blocks * rows + 2 * EDGE, cols), jnp.bfloat16),
@@ -204,15 +205,19 @@
             held[step] = lax.ppermute(held[step], ("side", "core"), pairs)
 
     face = jax.ShapeDtypeStruct((strip, Y), jnp.float32)
-    ends, low, high = pl.pallas_call(
+    ends, first, second = pl.pallas_call(
         functools.partial(outer_kernel, (strip, group)),
         out_shape=[jax.ShapeDtypeStruct((2, strip + EDGE, Y), jnp.float32), face, face],
         in_specs=[smem] + whole(group),
         out_specs=whole(3),
         compiler_params=params,
     )(spot, *outers)
-    under = lax.ppermute(high, "tile", [(t, t + 1) for t in range(tiles - 1)])
-    over = lax.ppermute(low, "tile", [(t + 1, t) for t in range(tiles - 1)])
+    swaps = []
+    for begin in range(2):
+        meet = [(t, t + 1) for t in range(begin, tiles - 1, 2)]
+        swaps.append(meet + [(b, a) for a, b in meet])
+    first = lax.ppermute(first, "tile", swaps[0])
+    second = lax.ppermute(second, "tile", swaps[1])
     return pl.pallas_call(
         functools.partial(laplace_kernel, (planes, strip, group)),
         out_shape=jax.ShapeDtypeStruct((planes * CORES, strip, Y), jnp.float32),
@@ -220,7 +225,7 @@
         out_specs=whole(1)[0],
         scratch_shapes=[pltpu.VMEM((planes * CORES, strip + EDGE, Y), jnp.float32)],
         compiler_params=params,
-    )(spot, ends, under, over, *inners)
+    )(spot, ends, first, second, *inners)
 
 
 def solution(mesh):

time: 60.7 us -> 58.4 us (0.962)
  the two profiles are of different devices: /device:TPU:3 before, /device:TPU:8 now
where the time goes in v5:
time: 58.4 us; the launch traced here: 58.1 us
  waiting for transfers between devices  35.9 us (61%)
  starting transfers between devices  14.4 us (25%)
  Pallas kernels  7.62 us (13%)
    all_to_all x1, waiting for transfers between devices, per_device(): lax.all_to_all(packed, ('tile', 'core'), split_axis=0, concat_axis=0, til...  25.3 us
    ppermute x6, waiting for transfers between devices, per_device(): held[step] = lax.ppermute(held[step], ('side', 'core'), pairs)  6.68 us
    all_to_all x1, starting transfers between devices, per_device(): lax.all_to_all(packed, ('tile', 'core'), split_axis=0, concat_axis=0, til...  6.28 us
    ppermute x6, starting transfers between devices, per_device(): held[step] = lax.ppermute(held[step], ('side', 'core'), pairs)  4.7 us
    ppermute x1, waiting for transfers between devices, per_device(): second = lax.ppermute(second, 'tile', swaps[1])  3.92 us
    pallas_call x1, Pallas kernels, per_device(): pl.pallas_call(pack_kernel, out_shape=jax.ShapeDtypeStruct((spread, block...  2.94 us
    pallas_call x1, Pallas kernels, per_device(): pl.pallas_call(functools.partial(place_kernel, (shots, times, planes, row...  2.56 us
    ppermute x1, starting transfers between devices, per_device(): second = lax.ppermute(second, 'tile', swaps[1])  1.91 us
  transfers between devices with their start and end apart: 9, of which 6 were waited for; matrix products, arithmetic and copies ran while one was open for 0% of the time, Pallas kernels for 1%

profile of v5, /device:TPU:8, one launch (start us, length us, event | category | flops | bytes accessed | tf_op | source)
XLA Modules:
  0.0 58.1 jit_solution(17632942217402396871)
XLA Ops:
  0.0 2.9 %shard_map.37 = bf16[16,272,128]{2,1,0:T(8,128)(2,1)} custom-call(s32[2,2]{1,0:T(2,128)} %corner_ref.1, bf16[2,1,16,64,128]{4,3,2,1,0:T(8,128)(2,1)} %bitcast.7, bf16[2,1,16,64,128]{4,3,2,1,0:T(8,128)(2,1)} %bitcast.8), custom_call_target="tpu_custom_call" | custom-call | tf_op jit(solution)/shard_map/pallas_call | solution.py:175
  3.0 6.3 %all-to-all-start = ((bf16[16,272,128]{2,1,0:T(8,128)(2,1)}), bf16[16,272,128]{2,1,0:T(8,128)(2,1)S(1)}, u32[]{:S(2)}, u32[]{:S(2)}) async-start(bf16[16,272,128]{2,1,0:T(8,128)(2,1)} %shard_map.37), calls=%async_computation | async-start | bytes 2228224 | tf_op jit(solution)/shard_map/all_to_all | solution.py:182
  9.2 0.1 pad_add_fusion.spot_ref
  9.3 25.3 %all-to-all-done.got_ref = bf16[16,272,128]{2,1,0:T(8,128)(2,1)S(1)} async-done(((bf16[16,272,128]{2,1,0:T(8,128)(2,1)}), bf16[16,272,128]{2,1,0:T(8,128)(2,1)S(1)}, u32[]{:S(2)}, u32[]{:S(2)}) %all-to-all-start) | async-done | bytes 1114144 | tf_op jit(solution)/shard_map/all_to_all | solution.py:182
  34.6 2.6 %shard_map.38 = (f32[2,1,72,256]{3,2,1,0:T(8,128)S(1)}, f32[2,1,72,256]{3,2,1,0:T(8,128)S(1)}, f32[2,1,72,256]{3,2,1,0:T(8,128)S(1)}, f32[2,1,72,256]{3,2,1,0:T(...) custom-call(s32[16,4]{1,0:T(8,128)S(1)} %bitcast.6, ...), custom_call_target="tpu_custom_call" | custom-call | tf_op jit(solution)/shard_map/pallas_call | solution.py:189
  37.2 1.0 %collective-permute-start = (f32[2,1,72,256]{3,2,1,0:T(8,128)S(1)}, f32[2,1,72,256]{3,2,1,0:T(8,128)S(1)}, u32[]{:S(2)}, u32[]{:S(2)}) collective-permute-start(f32[2,1,72,256]{3,2,1,0:T(8,128)S(1)} %get-tuple-element.17), channel_id=1, source_target_pairs={{0,8},{8,0},{16,24},{24,16},{1,9},{9,1},{17,25},{25,17},{2,10},{10... | collective-permute-start | bytes 442376 | tf_op jit(solution)/shard_map/ppermute | solution.py:205
  38.2 1.5 %collective-permute-start.1 = (f32[2,1,72,256]{3,2,1,0:T(8,128)S(1)}, f32[2,1,72,256]{3,2,1,0:T(8,128)S(1)}, u32[]{:S(2)}, u32[]{:S(2)}) collective-permute-start(f32[2,1,72,256]{3,2,1,0:T(8,128)S(1)} %get-tuple-element.18), channel_id=1, source_target_pairs={{0,16},{8,24},{16,0},{24,8},{1,17},{9,25},{17,1},{25,9},{2,18},{10... | collective-permute-start | bytes 442376 | tf_op jit(solution)/shard_map/ppermute | solution.py:205
  39.8 0.0 collective-permute-start.2
  39.8 0.6 %collective-permute-start.5 = (f32[2,1,72,256]{3,2,1,0:T(8,128)S(1)}, f32[2,1,72,256]{3,2,1,0:T(8,128)S(1)}, u32[]{:S(2)}, u32[]{:S(2)}) collective-permute-start(f32[2,1,72,256]{3,2,1,0:T(8,128)S(1)} %get-tuple-element.24), channel_id=1, source_target_pairs={{0,8},{8,0},{16,24},{24,16},{1,9},{9,1},{17,25},{25,17},{2,10},{10... | collective-permute-start | bytes 442376 | tf_op jit(solution)/shard_map/ppermute | solution.py:205
  40.4 1.5 %collective-permute-start.6 = (f32[2,1,72,256]{3,2,1,0:T(8,128)S(1)}, f32[2,1,72,256]{3,2,1,0:T(8,128)S(1)}, u32[]{:S(2)}, u32[]{:S(2)}) collective-permute-start(f32[2,1,72,256]{3,2,1,0:T(8,128)S(1)} %get-tuple-element.25), channel_id=1, source_target_pairs={{0,16},{8,24},{16,0},{24,8},{1,17},{9,25},{17,1},{25,9},{2,18},{10... | collective-permute-start | bytes 442376 | tf_op jit(solution)/shard_map/ppermute | solution.py:205
  41.9 0.0 collective-permute-done.refs_1_
  41.9 0.0 collective-permute-start.7
  41.9 3.1 %collective-permute-done.1.refs_2_ = f32[2,1,72,256]{3,2,1,0:T(8,128)S(1)} collective-permute-done((f32[2,1,72,256]{3,2,1,0:T(8,128)S(1)}, f32[2,1,72,256]{3,2,1,0:T(8,128)S(1)}, u32[]{:S(2)}, u32[]{:S(2)}) %collective-permute-start.1) | collective-permute-done | bytes 147488 | tf_op jit(solution)/shard_map/ppermute | solution.py:205
  45.0 2.2 %collective-permute-done.2.refs_3_ = f32[2,1,72,256]{3,2,1,0:T(8,128)S(1)} collective-permute-done((f32[2,1,72,256]{3,2,1,0:T(8,128)S(1)}, f32[2,1,72,256]{3,2,1,0:T(8,128)S(1)}, u32[]{:S(2)}, u32[]{:S(2)}) %collective-permute-start.2) | collective-permute-done | bytes 147488 | tf_op jit(solution)/shard_map/ppermute | solution.py:205
  47.2 0.6 %shard_map.39 = (f32[2,72,256]{2,1,0:T(8,128)S(1)}, f32[64,256]{1,0:T(8,128)S(1)}, f32[64,256]{1,0:T(8,128)S(1)}) custom-call(s32[3]{0:T(128)S(1)} %pad_add_fusion.spot_ref, f32[2,1,72,256]{3,2,1,0:T(8,128)S(1)} %get-tuple-element.16.refs_0_, f32[2,1,72,256]{3,2,1,0:T(8,128)S(1)} %collective-permute-done.refs_1_, ...), custom_call_target="tpu_custom_call" | custom-call | tf_op jit(solution)/shard_map/pallas_call | solution.py:208
  47.7 1.6 %collective-permute-start.3 = (f32[64,256]{1,0:T(8,128)S(1)}, f32[64,256]{1,0:T(8,128)S(1)}, u32[]{:S(2)}, u32[]{:S(2)}) collective-permute-start(f32[64,256]{1,0:T(8,128)S(1)} %get-tuple-element.21), channel_id=1, source_target_pairs={{0,1},{2,3},{4,5},{6,7},{1,0},{3,2},{5,4},{7,6},{8,9},{10,11},{12,... | collective-permute-start | bytes 196616 | tf_op jit(solution)/shard_map/ppermute | solution.py:219
  49.3 1.9 %collective-permute-start.4 = (f32[64,256]{1,0:T(8,128)S(1)}, f32[64,256]{1,0:T(8,128)S(1)}, u32[]{:S(2)}, u32[]{:S(2)}) collective-permute-start(f32[64,256]{1,0:T(8,128)S(1)} %get-tuple-element.22), channel_id=1, source_target_pairs={{1,2},{3,4},{5,6},{2,1},{4,3},{6,5},{9,10},{11,12},{13,14},{10,9},... | collective-permute-start | bytes 196616 | tf_op jit(solution)/shard_map/ppermute | solution.py:220
  51.2 0.0 collective-permute-done.5.refs_1_
  51.2 0.1 collective-permute-done.6.refs_2_
  51.3 1.4 %collective-permute-done.7.refs_3_ = f32[2,1,72,256]{3,2,1,0:T(8,128)S(1)} collective-permute-done((f32[2,1,72,256]{3,2,1,0:T(8,128)S(1)}, f32[2,1,72,256]{3,2,1,0:T(8,128)S(1)}, u32[]{:S(2)}, u32[]{:S(2)}) %collective-permute-start.7) | collective-permute-done | bytes 147488 | tf_op jit(solution)/shard_map/ppermute | solution.py:205
  52.7 0.0 collective-permute-done.3.first
  52.7 3.9 %collective-permute-done.4.second = f32[64,256]{1,0:T(8,128)S(1)} collective-permute-done((f32[64,256]{1,0:T(8,128)S(1)}, f32[64,256]{1,0:T(8,128)S(1)}, u32[]{:S(2)}, u32[]{:S(2)}) %collective-permute-start.4) | collective-permute-done | bytes 65568 | tf_op jit(solution)/shard_map/ppermute | solution.py:220
  56.6 1.5 %shard_map.40 = f32[4,64,256]{2,1,0:T(8,128)} custom-call(s32[3]{0:T(128)S(1)} %pad_add_fusion.spot_ref, f32[2,72,256]{2,1,0:T(8,128)S(1)} %get-tuple-element.20.ends, f32[64,256]{1,0:T(8,128)S(1)} %collective-permute-done.3.first, f32[64,256]{1,0:T(8,128)S(1)} %collective-permute-done.4.second, f32[2,1,72,256]{3,2,1,0:T(8,128)S(1)} %get-tuple-element.23.refs_0_, ...), custom_call_target="tpu_custom_call" | custom-call | tf_op jit(solution)/shard_map/pallas_call | solution.py:221
  (1 shorter events, 0.0 us)
Async XLA Ops:
  3.0 31.7 %all-to-all-start = ((bf16[16,272,128]{2,1,0:T(8,128)(2,1)}), bf16[16,272,128]{2,1,0:T(8,128)(2,1)S(1)}, u32[]{:S(2)}, u32[]{:S(2)}) async-start(bf16[16,272,128]{2,1,0:T(8,128)(2,1)} %shard_map.37), calls=%async_computation | async-start | bytes 2228224 | tf_op jit(solution)/shard_map/all_to_all | solution.py:182
  37.2 4.7 %collective-permute-start = (f32[2,1,72,256]{3,2,1,0:T(8,128)S(1)}, f32[2,1,72,256]{3,2,1,0:T(8,128)S(1)}, u32[]{:S(2)}, u32[]{:S(2)}) collective-permute-start(f32[2,1,72,256]{3,2,1,0:T(8,128)S(1)} %get-tuple-element.17), channel_id=1, source_target_pairs={{0,8},{8,0},{16,24},{24,16},{1,9},{9,1},{17,25},{25,17},{2,10},{10... | collective-permute-start | bytes 442376 | tf_op jit(solution)/shard_map/ppermute | solution.py:205
  38.2 6.7 %collective-permute-start.1 = (f32[2,1,72,256]{3,2,1,0:T(8,128)S(1)}, f32[2,1,72,256]{3,2,1,0:T(8,128)S(1)}, u32[]{:S(2)}, u32[]{:S(2)}) collective-permute-start(f32[2,1,72,256]{3,2,1,0:T(8,128)S(1)} %get-tuple-element.18), channel_id=1, source_target_pairs={{0,16},{8,24},{16,0},{24,8},{1,17},{9,25},{17,1},{25,9},{2,18},{10... | collective-permute-start | bytes 442376 | tf_op jit(solution)/shard_map/ppermute | solution.py:205
  39.8 7.4 %collective-permute-start.2 = (f32[2,1,72,256]{3,2,1,0:T(8,128)S(1)}, f32[2,1,72,256]{3,2,1,0:T(8,128)S(1)}, u32[]{:S(2)}, u32[]{:S(2)}) collective-permute-start(f32[2,1,72,256]{3,2,1,0:T(8,128)S(1)} %get-tuple-element.19), channel_id=1, source_target_pairs={{0,24},{8,16},{16,8},{24,0},{1,25},{9,17},{17,9},{25,1},{2,26},{10... | collective-permute-start | bytes 442376 | tf_op jit(solution)/shard_map/ppermute | solution.py:205
  39.8 11.5 %collective-permute-start.5 = (f32[2,1,72,256]{3,2,1,0:T(8,128)S(1)}, f32[2,1,72,256]{3,2,1,0:T(8,128)S(1)}, u32[]{:S(2)}, u32[]{:S(2)}) collective-permute-start(f32[2,1,72,256]{3,2,1,0:T(8,128)S(1)} %get-tuple-element.24), channel_id=1, source_target_pairs={{0,8},{8,0},{16,24},{24,16},{1,9},{9,1},{17,25},{25,17},{2,10},{10... | collective-permute-start | bytes 442376 | tf_op jit(solution)/shard_map/ppermute | solution.py:205
  40.4 10.9 %collective-permute-start.6 = (f32[2,1,72,256]{3,2,1,0:T(8,128)S(1)}, f32[2,1,72,256]{3,2,1,0:T(8,128)S(1)}, u32[]{:S(2)}, u32[]{:S(2)}) collective-permute-start(f32[2,1,72,256]{3,2,1,0:T(8,128)S(1)} %get-tuple-element.25), channel_id=1, source_target_pairs={{0,16},{8,24},{16,0},{24,8},{1,17},{9,25},{17,1},{25,9},{2,18},{10... | collective-permute-start | bytes 442376 | tf_op jit(solution)/shard_map/ppermute | solution.py:205
  41.9 10.8 %collective-permute-start.7 = (f32[2,1,72,256]{3,2,1,0:T(8,128)S(1)}, f32[2,1,72,256]{3,2,1,0:T(8,128)S(1)}, u32[]{:S(2)}, u32[]{:S(2)}) collective-permute-start(f32[2,1,72,256]{3,2,1,0:T(8,128)S(1)} %get-tuple-element.26), channel_id=1, source_target_pairs={{0,24},{8,16},{16,8},{24,0},{1,25},{9,17},{17,9},{25,1},{2,26},{10... | collective-permute-start | bytes 442376 | tf_op jit(solution)/shard_map/ppermute | solution.py:205
  47.7 4.9 %collective-permute-start.3 = (f32[64,256]{1,0:T(8,128)S(1)}, f32[64,256]{1,0:T(8,128)S(1)}, u32[]{:S(2)}, u32[]{:S(2)}) collective-permute-start(f32[64,256]{1,0:T(8,128)S(1)} %get-tuple-element.21), channel_id=1, source_target_pairs={{0,1},{2,3},{4,5},{6,7},{1,0},{3,2},{5,4},{7,6},{8,9},{10,11},{12,... | collective-permute-start | bytes 196616 | tf_op jit(solution)/shard_map/ppermute | solution.py:219
  49.3 7.3 %collective-permute-start.4 = (f32[64,256]{1,0:T(8,128)S(1)}, f32[64,256]{1,0:T(8,128)S(1)}, u32[]{:S(2)}, u32[]{:S(2)}) collective-permute-start(f32[64,256]{1,0:T(8,128)S(1)} %get-tuple-element.22), channel_id=1, source_target_pairs={{1,2},{3,4},{5,6},{2,1},{4,3},{6,5},{9,10},{11,12},{13,14},{10,9},... | collective-permute-start | bytes 196616 | tf_op jit(solution)/shard_map/ppermute | solution.py:220

commit v6 on v5

--- a/solution.py
+++ b/solution.py
@@ -196,7 +196,7 @@
     )(corner_all, spot, got)
     outers, inners = list(parts[::2]), list(parts[1::2])
     for held in (outers, inners):
-        for step in range(1, group):
+        for step in [*range(CORES, group), *range(1, CORES)]:
             pairs = [
                 (s * CORES + c, (s + step // CORES) % sides * CORES + (c + step) % CORES)
                 for s in range(sides)

time: 58.4 us -> 58.4 us (level)
  no operation moved by 1% of the time
where the time goes in v6:
time: 58.4 us; the launch traced here: 58.1 us
  waiting for transfers between devices  35.9 us (61%)
  starting transfers between devices  14.4 us (25%)
  Pallas kernels  7.62 us (13%)
    all_to_all x1, waiting for transfers between devices, per_device(): lax.all_to_all(packed, ('tile', 'core'), split_axis=0, concat_axis=0, til...  25.3 us
    ppermute x6, waiting for transfers between devices, per_device(): held[step] = lax.ppermute(held[step], ('side', 'core'), pairs)  6.68 us
    all_to_all x1, starting transfers between devices, per_device(): lax.all_to_all(packed, ('tile', 'core'), split_axis=0, concat_axis=0, til...  6.28 us
    ppermute x6, starting transfers between devices, per_device(): held[step] = lax.ppermute(held[step], ('side', 'core'), pairs)  4.7 us
    ppermute x1, waiting for transfers between devices, per_device(): second = lax.ppermute(second, 'tile', swaps[1])  3.92 us
    pallas_call x1, Pallas kernels, per_device(): pl.pallas_call(pack_kernel, out_shape=jax.ShapeDtypeStruct((spread, block...  2.94 us
    pallas_call x1, Pallas kernels, per_device(): pl.pallas_call(functools.partial(place_kernel, (shots, times, planes, row...  2.56 us
    ppermute x1, starting transfers between devices, per_device(): second = lax.ppermute(second, 'tile', swaps[1])  1.91 us
  transfers between devices with their start and end apart: 9, of which 6 were waited for; matrix products, arithmetic and copies ran while one was open for 0% of the time, Pallas kernels for 1%

profile of v6, /device:TPU:8, one launch (start us, length us, event | category | flops | bytes accessed | tf_op | source)
XLA Modules:
  0.0 58.1 jit_solution(17632942217402396871)
XLA Ops:
  0.0 2.9 %shard_map.37 = bf16[16,272,128]{2,1,0:T(8,128)(2,1)} custom-call(s32[2,2]{1,0:T(2,128)} %corner_ref.1, bf16[2,1,16,64,128]{4,3,2,1,0:T(8,128)(2,1)} %bitcast.7, bf16[2,1,16,64,128]{4,3,2,1,0:T(8,128)(2,1)} %bitcast.8), custom_call_target="tpu_custom_call" | custom-call | tf_op jit(solution)/shard_map/pallas_call | solution.py:175
  3.0 6.3 %all-to-all-start = ((bf16[16,272,128]{2,1,0:T(8,128)(2,1)}), bf16[16,272,128]{2,1,0:T(8,128)(2,1)S(1)}, u32[]{:S(2)}, u32[]{:S(2)}) async-start(bf16[16,272,128]{2,1,0:T(8,128)(2,1)} %shard_map.37), calls=%async_computation | async-start | bytes 2228224 | tf_op jit(solution)/shard_map/all_to_all | solution.py:182
  9.2 0.1 pad_add_fusion.spot_ref
  9.3 25.3 %all-to-all-done.got_ref = bf16[16,272,128]{2,1,0:T(8,128)(2,1)S(1)} async-done(((bf16[16,272,128]{2,1,0:T(8,128)(2,1)}), bf16[16,272,128]{2,1,0:T(8,128)(2,1)S(1)}, u32[]{:S(2)}, u32[]{:S(2)}) %all-to-all-start) | async-done | bytes 1114144 | tf_op jit(solution)/shard_map/all_to_all | solution.py:182
  34.6 2.6 %shard_map.38 = (f32[2,1,72,256]{3,2,1,0:T(8,128)S(1)}, f32[2,1,72,256]{3,2,1,0:T(8,128)S(1)}, f32[2,1,72,256]{3,2,1,0:T(8,128)S(1)}, f32[2,1,72,256]{3,2,1,0:T(...) custom-call(s32[16,4]{1,0:T(8,128)S(1)} %bitcast.6, ...), custom_call_target="tpu_custom_call" | custom-call | tf_op jit(solution)/shard_map/pallas_call | solution.py:189
  37.2 1.0 %collective-permute-start = (f32[2,1,72,256]{3,2,1,0:T(8,128)S(1)}, f32[2,1,72,256]{3,2,1,0:T(8,128)S(1)}, u32[]{:S(2)}, u32[]{:S(2)}) collective-permute-start(f32[2,1,72,256]{3,2,1,0:T(8,128)S(1)} %get-tuple-element.17), channel_id=1, source_target_pairs={{0,8},{8,0},{16,24},{24,16},{1,9},{9,1},{17,25},{25,17},{2,10},{10... | collective-permute-start | bytes 442376 | tf_op jit(solution)/shard_map/ppermute | solution.py:205
  38.2 1.5 %collective-permute-start.1 = (f32[2,1,72,256]{3,2,1,0:T(8,128)S(1)}, f32[2,1,72,256]{3,2,1,0:T(8,128)S(1)}, u32[]{:S(2)}, u32[]{:S(2)}) collective-permute-start(f32[2,1,72,256]{3,2,1,0:T(8,128)S(1)} %get-tuple-element.18), channel_id=1, source_target_pairs={{0,16},{8,24},{16,0},{24,8},{1,17},{9,25},{17,1},{25,9},{2,18},{10... | collective-permute-start | bytes 442376 | tf_op jit(solution)/shard_map/ppermute | solution.py:205
  39.8 0.0 collective-permute-start.2
  39.8 0.6 %collective-permute-start.5 = (f32[2,1,72,256]{3,2,1,0:T(8,128)S(1)}, f32[2,1,72,256]{3,2,1,0:T(8,128)S(1)}, u32[]{:S(2)}, u32[]{:S(2)}) collective-permute-start(f32[2,1,72,256]{3,2,1,0:T(8,128)S(1)} %get-tuple-element.24), channel_id=1, source_target_pairs={{0,8},{8,0},{16,24},{24,16},{1,9},{9,1},{17,25},{25,17},{2,10},{10... | collective-permute-start | bytes 442376 | tf_op jit(solution)/shard_map/ppermute | solution.py:205
  40.4 1.5 %collective-permute-start.6 = (f32[2,1,72,256]{3,2,1,0:T(8,128)S(1)}, f32[2,1,72,256]{3,2,1,0:T(8,128)S(1)}, u32[]{:S(2)}, u32[]{:S(2)}) collective-permute-start(f32[2,1,72,256]{3,2,1,0:T(8,128)S(1)} %get-tuple-element.25), channel_id=1, source_target_pairs={{0,16},{8,24},{16,0},{24,8},{1,17},{9,25},{17,1},{25,9},{2,18},{10... | collective-permute-start | bytes 442376 | tf_op jit(solution)/shard_map/ppermute | solution.py:205
  41.9 0.0 collective-permute-done.refs_1_
  41.9 0.0 collective-permute-start.7
  41.9 3.1 %collective-permute-done.1.refs_2_ = f32[2,1,72,256]{3,2,1,0:T(8,128)S(1)} collective-permute-done((f32[2,1,72,256]{3,2,1,0:T(8,128)S(1)}, f32[2,1,72,256]{3,2,1,0:T(8,128)S(1)}, u32[]{:S(2)}, u32[]{:S(2)}) %collective-permute-start.1) | collective-permute-done | bytes 147488 | tf_op jit(solution)/shard_map/ppermute | solution.py:205
  45.0 2.2 %collective-permute-done.2.refs_3_ = f32[2,1,72,256]{3,2,1,0:T(8,128)S(1)} collective-permute-done((f32[2,1,72,256]{3,2,1,0:T(8,128)S(1)}, f32[2,1,72,256]{3,2,1,0:T(8,128)S(1)}, u32[]{:S(2)}, u32[]{:S(2)}) %collective-permute-start.2) | collective-permute-done | bytes 147488 | tf_op jit(solution)/shard_map/ppermute | solution.py:205
  47.2 0.6 %shard_map.39 = (f32[2,72,256]{2,1,0:T(8,128)S(1)}, f32[64,256]{1,0:T(8,128)S(1)}, f32[64,256]{1,0:T(8,128)S(1)}) custom-call(s32[3]{0:T(128)S(1)} %pad_add_fusion.spot_ref, f32[2,1,72,256]{3,2,1,0:T(8,128)S(1)} %get-tuple-element.16.refs_0_, f32[2,1,72,256]{3,2,1,0:T(8,128)S(1)} %collective-permute-done.refs_1_, ...), custom_call_target="tpu_custom_call" | custom-call | tf_op jit(solution)/shard_map/pallas_call | solution.py:208
  47.7 1.6 %collective-permute-start.3 = (f32[64,256]{1,0:T(8,128)S(1)}, f32[64,256]{1,0:T(8,128)S(1)}, u32[]{:S(2)}, u32[]{:S(2)}) collective-permute-start(f32[64,256]{1,0:T(8,128)S(1)} %get-tuple-element.21), channel_id=1, source_target_pairs={{0,1},{2,3},{4,5},{6,7},{1,0},{3,2},{5,4},{7,6},{8,9},{10,11},{12,... | collective-permute-start | bytes 196616 | tf_op jit(solution)/shard_map/ppermute | solution.py:219
  49.3 1.9 %collective-permute-start.4 = (f32[64,256]{1,0:T(8,128)S(1)}, f32[64,256]{1,0:T(8,128)S(1)}, u32[]{:S(2)}, u32[]{:S(2)}) collective-permute-start(f32[64,256]{1,0:T(8,128)S(1)} %get-tuple-element.22), channel_id=1, source_target_pairs={{1,2},{3,4},{5,6},{2,1},{4,3},{6,5},{9,10},{11,12},{13,14},{10,9},... | collective-permute-start | bytes 196616 | tf_op jit(solution)/shard_map/ppermute | solution.py:220
  51.2 0.0 collective-permute-done.5.refs_1_
  51.2 0.1 collective-permute-done.6.refs_2_
  51.3 1.4 %collective-permute-done.7.refs_3_ = f32[2,1,72,256]{3,2,1,0:T(8,128)S(1)} collective-permute-done((f32[2,1,72,256]{3,2,1,0:T(8,128)S(1)}, f32[2,1,72,256]{3,2,1,0:T(8,128)S(1)}, u32[]{:S(2)}, u32[]{:S(2)}) %collective-permute-start.7) | collective-permute-done | bytes 147488 | tf_op jit(solution)/shard_map/ppermute | solution.py:205
  52.7 0.0 collective-permute-done.3.first
  52.7 3.9 %collective-permute-done.4.second = f32[64,256]{1,0:T(8,128)S(1)} collective-permute-done((f32[64,256]{1,0:T(8,128)S(1)}, f32[64,256]{1,0:T(8,128)S(1)}, u32[]{:S(2)}, u32[]{:S(2)}) %collective-permute-start.4) | collective-permute-done | bytes 65568 | tf_op jit(solution)/shard_map/ppermute | solution.py:220
  56.6 1.5 %shard_map.40 = f32[4,64,256]{2,1,0:T(8,128)} custom-call(s32[3]{0:T(128)S(1)} %pad_add_fusion.spot_ref, f32[2,72,256]{2,1,0:T(8,128)S(1)} %get-tuple-element.20.ends, f32[64,256]{1,0:T(8,128)S(1)} %collective-permute-done.3.first, f32[64,256]{1,0:T(8,128)S(1)} %collective-permute-done.4.second, f32[2,1,72,256]{3,2,1,0:T(8,128)S(1)} %get-tuple-element.23.refs_0_, ...), custom_call_target="tpu_custom_call" | custom-call | tf_op jit(solution)/shard_map/pallas_call | solution.py:221
  (1 shorter events, 0.0 us)
Async XLA Ops:
  3.0 31.7 %all-to-all-start = ((bf16[16,272,128]{2,1,0:T(8,128)(2,1)}), bf16[16,272,128]{2,1,0:T(8,128)(2,1)S(1)}, u32[]{:S(2)}, u32[]{:S(2)}) async-start(bf16[16,272,128]{2,1,0:T(8,128)(2,1)} %shard_map.37), calls=%async_computation | async-start | bytes 2228224 | tf_op jit(solution)/shard_map/all_to_all | solution.py:182
  37.2 4.7 %collective-permute-start = (f32[2,1,72,256]{3,2,1,0:T(8,128)S(1)}, f32[2,1,72,256]{3,2,1,0:T(8,128)S(1)}, u32[]{:S(2)}, u32[]{:S(2)}) collective-permute-start(f32[2,1,72,256]{3,2,1,0:T(8,128)S(1)} %get-tuple-element.17), channel_id=1, source_target_pairs={{0,8},{8,0},{16,24},{24,16},{1,9},{9,1},{17,25},{25,17},{2,10},{10... | collective-permute-start | bytes 442376 | tf_op jit(solution)/shard_map/ppermute | solution.py:205
  38.2 6.7 %collective-permute-start.1 = (f32[2,1,72,256]{3,2,1,0:T(8,128)S(1)}, f32[2,1,72,256]{3,2,1,0:T(8,128)S(1)}, u32[]{:S(2)}, u32[]{:S(2)}) collective-permute-start(f32[2,1,72,256]{3,2,1,0:T(8,128)S(1)} %get-tuple-element.18), channel_id=1, source_target_pairs={{0,16},{8,24},{16,0},{24,8},{1,17},{9,25},{17,1},{25,9},{2,18},{10... | collective-permute-start | bytes 442376 | tf_op jit(solution)/shard_map/ppermute | solution.py:205
  39.8 7.4 %collective-permute-start.2 = (f32[2,1,72,256]{3,2,1,0:T(8,128)S(1)}, f32[2,1,72,256]{3,2,1,0:T(8,128)S(1)}, u32[]{:S(2)}, u32[]{:S(2)}) collective-permute-start(f32[2,1,72,256]{3,2,1,0:T(8,128)S(1)} %get-tuple-element.19), channel_id=1, source_target_pairs={{0,24},{8,16},{16,8},{24,0},{1,25},{9,17},{17,9},{25,1},{2,26},{10... | collective-permute-start | bytes 442376 | tf_op jit(solution)/shard_map/ppermute | solution.py:205
  39.8 11.5 %collective-permute-start.5 = (f32[2,1,72,256]{3,2,1,0:T(8,128)S(1)}, f32[2,1,72,256]{3,2,1,0:T(8,128)S(1)}, u32[]{:S(2)}, u32[]{:S(2)}) collective-permute-start(f32[2,1,72,256]{3,2,1,0:T(8,128)S(1)} %get-tuple-element.24), channel_id=1, source_target_pairs={{0,8},{8,0},{16,24},{24,16},{1,9},{9,1},{17,25},{25,17},{2,10},{10... | collective-permute-start | bytes 442376 | tf_op jit(solution)/shard_map/ppermute | solution.py:205
  40.4 10.9 %collective-permute-start.6 = (f32[2,1,72,256]{3,2,1,0:T(8,128)S(1)}, f32[2,1,72,256]{3,2,1,0:T(8,128)S(1)}, u32[]{:S(2)}, u32[]{:S(2)}) collective-permute-start(f32[2,1,72,256]{3,2,1,0:T(8,128)S(1)} %get-tuple-element.25), channel_id=1, source_target_pairs={{0,16},{8,24},{16,0},{24,8},{1,17},{9,25},{17,1},{25,9},{2,18},{10... | collective-permute-start | bytes 442376 | tf_op jit(solution)/shard_map/ppermute | solution.py:205
  41.9 10.8 %collective-permute-start.7 = (f32[2,1,72,256]{3,2,1,0:T(8,128)S(1)}, f32[2,1,72,256]{3,2,1,0:T(8,128)S(1)}, u32[]{:S(2)}, u32[]{:S(2)}) collective-permute-start(f32[2,1,72,256]{3,2,1,0:T(8,128)S(1)} %get-tuple-element.26), channel_id=1, source_target_pairs={{0,24},{8,16},{16,8},{24,0},{1,25},{9,17},{17,9},{25,1},{2,26},{10... | collective-permute-start | bytes 442376 | tf_op jit(solution)/shard_map/ppermute | solution.py:205
  47.7 4.9 %collective-permute-start.3 = (f32[64,256]{1,0:T(8,128)S(1)}, f32[64,256]{1,0:T(8,128)S(1)}, u32[]{:S(2)}, u32[]{:S(2)}) collective-permute-start(f32[64,256]{1,0:T(8,128)S(1)} %get-tuple-element.21), channel_id=1, source_target_pairs={{0,1},{2,3},{4,5},{6,7},{1,0},{3,2},{5,4},{7,6},{8,9},{10,11},{12,... | collective-permute-start | bytes 196616 | tf_op jit(solution)/shard_map/ppermute | solution.py:219
  49.3 7.3 %collective-permute-start.4 = (f32[64,256]{1,0:T(8,128)S(1)}, f32[64,256]{1,0:T(8,128)S(1)}, u32[]{:S(2)}, u32[]{:S(2)}) collective-permute-start(f32[64,256]{1,0:T(8,128)S(1)} %get-tuple-element.22), channel_id=1, source_target_pairs={{1,2},{3,4},{5,6},{2,1},{4,3},{6,5},{9,10},{11,12},{13,14},{10,9},... | collective-permute-start | bytes 196616 | tf_op jit(solution)/shard_map/ppermute | solution.py:220
